TPU v7x, 64 devices: a 2x2x8 block of a 4x4x8 slice. The times are simulated.
64 devices in a mesh: req: 4 (over x, y), cp: 16 (over z, core).
Axes of the slice: x: 2, y: 2, z: 8, core: 2. Of those that a mesh axis runs over, the one named last changes fastest.
The devices are a block of a 4x4x8 slice.
Arguments:
- hidden: bfloat16 [8192, 2048], P(('req', 'cp')), parts along dimension 0
- positions: int32 [8192], P(('req', 'cp')), parts along dimension 0
- segments: int32 [8192], P(('req', 'cp')), parts along dimension 0
- gain_1: bfloat16 [3, 2048], replicated
- gain_2: bfloat16 [3, 2048], replicated
- w_q: bfloat16 [3, 2048, 32, 64], replicated
- w_k: bfloat16 [3, 2048, 8, 64], replicated
- w_v: bfloat16 [3, 2048, 8, 64], replicated
- w_o: bfloat16 [3, 32, 64, 2048], replicated
- w_1: bfloat16 [3, 2048, 8192], replicated
- w_3: bfloat16 [3, 2048, 8192], replicated
- w_2: bfloat16 [3, 8192, 2048], replicated
Outputs:
- output 1: bfloat16 [8192, 2048], P(('req', 'cp')), parts along dimension 0
- output 2: bfloat16 [3, 8192, 512], P(None, 'req', 'cp'), parts along dimension 1
- output 3: bfloat16 [3, 8192, 512], P(None, 'req', 'cp'), parts along dimension 1
There are 4 independent parts. A program takes and returns all parts, laid end to end along the dimension named above; an argument that names none is the same for every part.
All inputs are finite; a program needn't handle non-finite values.
Results may differ from a plain program's by a relative error of at most 0.02.
Values are sent between devices in bfloat16 or wider.
A program may use at most 768 MiB of HBM per device.

v0:
```python
import jax
import jax.numpy as jnp
from jax import lax
from jax.sharding import PartitionSpec as P, NamedSharding

NORM_EPS = 1e-5
ROPE_THETA = 10000.0
MASK_FILL = -1e30


def rms_norm(residual, gain_row):
    resid_f32 = residual.astype(jnp.float32)
    inv_rms = lax.rsqrt(jnp.mean(resid_f32 * resid_f32, axis=-1, keepdims=True) + NORM_EPS)
    return (resid_f32 * inv_rms * gain_row.astype(jnp.float32)).astype(jnp.bfloat16)


def rope_tables(positions, head_dim):
    inv_freq = ROPE_THETA ** (-2.0 * jnp.arange(head_dim // 2, dtype=jnp.float32) / head_dim)
    rot_angle = positions.astype(jnp.float32)[..., None] * inv_freq
    return jnp.cos(rot_angle), jnp.sin(rot_angle)


def apply_rope(proj, cos_t, sin_t):
    half_dim = proj.shape[-1] // 2
    front_half = proj[..., :half_dim]
    back_half = proj[..., half_dim:]
    cos_b = cos_t[..., None, :]
    sin_b = sin_t[..., None, :]
    return jnp.concatenate([front_half * cos_b - back_half * sin_b, back_half * cos_b + front_half * sin_b], axis=-1)


def mlp_block(residual, gain_row, w_up1, w_up3, w_down):
    normed = rms_norm(residual, gain_row)
    gate_pre = jnp.dot(normed, w_up1, preferred_element_type=jnp.float32)
    up_pre = jnp.dot(normed, w_up3, preferred_element_type=jnp.float32)
    gated_act = (jax.nn.silu(gate_pre) * up_pre).astype(jnp.bfloat16)
    return (residual.astype(jnp.float32) + jnp.dot(gated_act, w_down, preferred_element_type=jnp.float32)).astype(jnp.bfloat16)


def local_attention(q_rot, k_full, v_full, allowed):
    n_tok, n_heads, head_dim = q_rot.shape
    n_kv = k_full.shape[1]
    q_grp = q_rot.reshape(n_tok, n_kv, n_heads // n_kv, head_dim)
    scores = jnp.einsum('tkgd,skd->kgts', q_grp, k_full, preferred_element_type=jnp.float32) * head_dim ** -0.5
    scores = jnp.where(allowed, scores, MASK_FILL)
    row_max = jnp.max(scores, axis=-1, keepdims=True)
    exp_scores = jnp.exp(scores - row_max)
    attn_prob = (exp_scores / jnp.sum(exp_scores, axis=-1, keepdims=True)).astype(jnp.bfloat16)
    attn_out = jnp.einsum('kgts,skd->tkgd', attn_prob, v_full, preferred_element_type=jnp.float32)
    return attn_out.astype(jnp.bfloat16).reshape(n_tok, n_heads, head_dim)


def to_natural(cache_rows, n_cp):
    n_layers, seq_len, n_cols = cache_rows.shape
    half_len = seq_len // (2 * n_cp)
    blocks = cache_rows.reshape(n_layers, n_cp, 2, half_len, n_cols)
    front_part = blocks[:, :, 0]
    back_part = jnp.flip(blocks[:, :, 1], axis=1)
    return jnp.concatenate([front_part, back_part], axis=1).reshape(n_layers, seq_len, n_cols)


def solution(mesh):
    n_cp = mesh.shape['cp']
    row_spec = P(('req', 'cp'), None)
    tok_spec = P(('req', 'cp'))
    rep_spec = P()
    cache_spec = P(None, 'req', 'cp')

    def local_step(hidden, positions, segments, gain_1, gain_2, w_q, w_k, w_v, w_o, w_1, w_3, w_2):
        n_layers = w_q.shape[0]
        head_dim = w_q.shape[3]
        n_kv = w_k.shape[2]
        n_tok = hidden.shape[0]
        kv_width = n_kv * head_dim
        all_pos = lax.all_gather(positions, 'cp', tiled=True)
        all_seg = lax.all_gather(segments, 'cp', tiled=True)
        allowed = (segments[:, None] == all_seg[None, :]) & (all_pos[None, :] <= positions[:, None])
        cos_t, sin_t = rope_tables(positions, head_dim)
        residual = hidden
        k_keep = []
        v_keep = []
        for layer_idx in range(n_layers):
            normed = rms_norm(residual, gain_1[layer_idx])
            q_rot = apply_rope(jnp.einsum('td,dhe->the', normed, w_q[layer_idx], preferred_element_type=jnp.float32), cos_t, sin_t).astype(jnp.bfloat16)
            k_rot = apply_rope(jnp.einsum('td,dhe->the', normed, w_k[layer_idx], preferred_element_type=jnp.float32), cos_t, sin_t).astype(jnp.bfloat16)
            v_new = jnp.einsum('td,dhe->the', normed, w_v[layer_idx], preferred_element_type=jnp.float32).astype(jnp.bfloat16)
            k_full = lax.all_gather(k_rot, 'cp', tiled=True)
            v_full = lax.all_gather(v_new, 'cp', tiled=True)
            attn_out = local_attention(q_rot, k_full, v_full, allowed)
            residual = (residual.astype(jnp.float32) + jnp.einsum('the,hed->td', attn_out, w_o[layer_idx], preferred_element_type=jnp.float32)).astype(jnp.bfloat16)
            residual = mlp_block(residual, gain_2[layer_idx], w_1[layer_idx], w_3[layer_idx], w_2[layer_idx])
            k_keep.append(k_rot.reshape(n_tok, kv_width))
            v_keep.append(v_new.reshape(n_tok, kv_width))
        k_cache = lax.all_to_all(jnp.stack(k_keep), 'cp', 2, 1, tiled=True)
        v_cache = lax.all_to_all(jnp.stack(v_keep), 'cp', 2, 1, tiled=True)
        return residual, to_natural(k_cache, n_cp), to_natural(v_cache, n_cp)

    return jax.shard_map(
        local_step,
        mesh=mesh,
        in_specs=(row_spec, tok_spec, tok_spec) + (rep_spec,) * 9,
        out_specs=(row_spec, cache_spec, cache_spec),
        check_vma=False,
    )
```

profile of v0, /device:TPU:21, one launch (start us, length us, event | category | flops | bytes accessed | tf_op | source)
XLA Modules:
  0.0 471.7 jit_solution(18250670783897405715)
XLA Ops:
  7.3 1.4 slice_convert_fusion.1
  8.7 5.1 %fusion.315 = (bf16[1,2048,8,64]{1,3,2,0:T(8,128)(2,1)}, bf16[1,2048,8,64]{1,3,2,0:T(8,128)(2,1)S(1)}, bf16[1,2048,8,64]{1,3,2,0:T(8,128)(2,1)S(1)}) fusion(bf16[3,2048,8,64]{1,3,2,0:T(8,128)(2,1)} %param.18), kind=kLoop, calls=%fused_computation.216 | loop fusion | bytes 12582912 | tf_op jit(solution)/shard_map/slice | solution.py:85
  14.2 0.8 fusion.309
  15.1 0.7 maximum_convert_fusion
  15.9 6.1 %fusion.314 = (bf16[1,2048,8,64]{1,3,2,0:T(8,128)(2,1)}, bf16[1,2048,8,64]{1,3,2,0:T(8,128)(2,1)S(1)}, bf16[1,2048,8,64]{1,3,2,0:T(8,128)(2,1)}) fusion(bf16[3,2048,8,64]{1,3,2,0:T(8,128)(2,1)} %param.19), kind=kLoop, calls=%fused_computation.215 | loop fusion | bytes 12582912 | tf_op jit(solution)/shard_map/slice | solution.py:86
  21.9 0.8 fusion.311
  22.7 0.7 convert_element_type.167
  23.5 14.7 %fusion.313 = (bf16[1,2048,32,64]{1,3,2,0:T(8,128)(2,1)}, bf16[1,2048,32,64]{1,3,2,0:T(8,128)(2,1)S(1)}, bf16[1,2048,32,64]{1,3,2,0:T(8,128)(2,1)}) fusion(bf16[3,2048,32,64]{1,3,2,0:T(8,128)(2,1)} %param.17), kind=kLoop, calls=%fused_computation.214 | loop fusion | bytes 50331648 | tf_op jit(solution)/shard_map/slice | solution.py:84
  38.2 22.7 %all-gather = s32[16,1,128]{2,1,0:T(1,128)S(1)} all-gather(s32[1,1,128]{2,1,0:T(1,128)S(1)} %bitcast.483), channel_id=1, replica_groups=mesh['req'=4,'cp'=16] {'cp'}, dimensions={0}, use_global_device_ids=true | all-gather | bytes 8704 | tf_op jit(solution)/shard_map/all_gather | solution.py:76
  61.0 15.1 %all-gather.1 = s32[16,1,128]{2,1,0:T(1,128)S(1)} all-gather(s32[1,1,128]{2,1,0:T(1,128)S(1)} %bitcast.482), channel_id=1, replica_groups=mesh['req'=4,'cp'=16] {'cp'}, dimensions={0}, use_global_device_ids=true | all-gather | bytes 8704 | tf_op jit(solution)/shard_map/all_gather | solution.py:75
  76.1 2.5 fusion.307
  78.7 0.6 slice_convert_fusion
  79.3 1.3 compare_and_fusion
  80.7 12.6 %fusion.318 = f32[8,4,128]{2,1,0:T(4,128)S(1)} fusion(pred[128,2048]{0,1:T(8,128)(4,1)S(1)} %compare_and_fusion, bf16[2048,8,64]{0,2,1:T(8,128)(2,1)} %all-gather.11.cloned.1.call-done, bf16[128,8,4,32]{0,3,2,1:T(8,128)(2,1)S(1)} %bitcast.466, bf16[128,8,4,32]{0,3,2,1:T(8,128)(2,1)S(1)} %bitcast.464), kind=kOutput, calls=%fused_computation.219 | convolution fusion | flops 1108346880 | bytes 2899968 | tf_op jit(solution)/shard_map/sub | solution.py:47
  93.3 3.4 all-gather.9.cloned.1.call-done
  96.7 17.6 %fusion.229 = bf16[8,64,4,128]{3,1,2,0:T(8,128)(2,1)} fusion(f32[8,4,128]{2,1,0:T(4,128)S(1)} %fusion.318, pred[128,2048]{0,1:T(8,128)(4,1)S(1)} %compare_and_fusion, bf16[2048,8,64]{0,2,1:T(8,128)(2,1)} %all-gather.11.cloned.1.call-done, bf16[2048,8,64]{0,2,1:T(8,128)(2,1)} %all-gather.9.cloned.1.call-done, bf16[128,8,4,32]{0,3,2,1:T(8,128)(2,1)S(1)} %bitcast.467, ...), kind=kOutput, calls=%fused_computation.114 | convolution fusion | flops 2190743552 | bytes 5521408 | tf_op jit(solution)/shard_map/kgts,skd->tkgd/dot_general | solution.py:49
  114.3 5.8 %multiply_reduce_fusion.4 = (f32[128]{0:T(128)S(1)}, f32[128,2048]{1,0:T(8,128)}) fusion(bf16[128,32,64]{0,2,1:T(8,128)(2,1)} %bitcast.484, bf16[3,32,64,2048]{3,2,1,0:T(8,128)(2,1)} %param.20, bf16[128,2048]{1,0:T(8,128)(2,1)S(1)} %copy-done), kind=kOutput, calls=%fused_computation.127 | convolution fusion | flops 1075314560 | bytes 10486272 | tf_op jit(solution)/shard_map/the,hed->td/dot_general | solution.py:90
  120.1 15.4 %fusion.19 = f32[128,8192]{1,0:T(8,128)} fusion(bf16[3,2048,8192]{2,1,0:T(8,128)(2,1)} %param.21, f32[128,2048]{1,0:T(8,128)} %get-tuple-element.37, f32[2048]{0:T(1024)S(1)} %bitcast.480, f32[128]{0:T(128)S(1)} %add_rsqrt_fusion.4), kind=kOutput, calls=%fused_computation.21 | convolution fusion | flops 4295753728 | bytes 38806016 | tf_op jit(solution)/shard_map/dot_general | solution.py:34
  135.5 29.7 %multiply_reduce_fusion.3 = (f32[128]{0:T(128)S(1)}, f32[128,2048]{1,0:T(8,128)}) fusion(f32[128,2048]{1,0:T(8,128)} %get-tuple-element.37, bf16[3,8192,2048]{2,1,0:T(8,128)(2,1)} %param.23, bf16[3,2048,8192]{2,1,0:T(8,128)(2,1)} %param.22, f32[128,8192]{1,0:T(8,128)} %fusion.19, f32[2048]{0:T(1024)S(1)} %bitcast.481, f32[128]{0:T(128)S(1)} %add_rsqrt_fusion.4), kind=kOutput, calls=%fused_computation.125 | convolution fusion | flops 8598323200 | bytes 74458112 | tf_op jit(solution)/shard_map/dot_general | solution.py:37
  165.2 1.4 multiply_convert_fusion.3
  166.6 0.7 fusion.338
  167.4 0.7 maximum_convert_fusion.1
  168.2 2.3 fusion.337
  170.5 0.7 convert_element_type.180
  171.3 5.8 %fusion.339 = f32[128,2048]{0,1:S(1)} fusion(bf16[128,2048]{1,0:T(8,128)(2,1)S(1)} %multiply_convert_fusion.3, bf16[2048,2048]{0,1:T(8,128)(2,1)} %bitcast.428), kind=kOutput, calls=%fused_computation.224 | convolution fusion | flops 1073741824 | bytes 9961472
  177.2 27.3 %all-gather.15.cloned.1.call-done = bf16[2048,8,64]{0,2,1:T(8,128)(2,1)} async-done(((bf16[128,8,64]{0,2,1:T(8,128)(2,1)}), bf16[2048,8,64]{0,2,1:T(8,128)(2,1)}) %all-gather.15.cloned.1.call-update) | async-done | bytes 2097168 | tf_op jit(solution)/shard_map/all_gather | solution.py:87
  204.5 12.6 %fusion.325 = f32[8,4,128]{2,1,0:T(4,128)S(1)} fusion(pred[128,2048]{0,1:T(8,128)(4,1)S(1)} %compare_and_fusion, bf16[2048,8,64]{0,2,1:T(8,128)(2,1)} %all-gather.15.cloned.1.call-done, bf16[128,8,4,32]{0,3,2,1:T(8,128)(2,1)S(1)} %bitcast.470, bf16[128,8,4,32]{0,3,2,1:T(8,128)(2,1)S(1)} %bitcast.468), kind=kOutput, calls=%fused_computation.220 | convolution fusion | flops 1108346880 | bytes 2899968 | tf_op jit(solution)/shard_map/sub | solution.py:47
  217.1 25.0 %all-gather.13.cloned.1.call-done = bf16[2048,8,64]{0,2,1:T(8,128)(2,1)} async-done(((bf16[128,8,64]{0,2,1:T(8,128)(2,1)}), bf16[2048,8,64]{0,2,1:T(8,128)(2,1)}) %all-gather.13.cloned.1.call-update) | async-done | bytes 2097168 | tf_op jit(solution)/shard_map/all_gather | solution.py:88
  242.2 17.1 %fusion.220 = bf16[8,64,4,128]{3,1,2,0:T(8,128)(2,1)S(1)} fusion(f32[8,4,128]{2,1,0:T(4,128)S(1)} %fusion.325, pred[128,2048]{0,1:T(8,128)(4,1)S(1)} %compare_and_fusion, bf16[2048,8,64]{0,2,1:T(8,128)(2,1)} %all-gather.15.cloned.1.call-done, bf16[2048,8,64]{0,2,1:T(8,128)(2,1)} %all-gather.13.cloned.1.call-done, ...), kind=kOutput, calls=%fused_computation.113 | convolution fusion | flops 2190743552 | bytes 5521408 | tf_op jit(solution)/shard_map/kgts,skd->tkgd/dot_general | solution.py:49
  259.3 4.7 %multiply_reduce_fusion.2 = (f32[128]{0:T(128)S(1)}, f32[128,2048]{1,0:T(8,128)S(1)}) fusion(f32[128,2048]{1,0:T(8,128)S(1)} %copy-done.3, bf16[128,32,64]{0,2,1:T(8,128)(2,1)S(1)} %bitcast.456, bf16[3,32,64,2048]{3,2,1,0:T(8,128)(2,1)} %param.20), kind=kOutput, calls=%fused_computation.123 | convolution fusion | flops 1075052416 | bytes 11010560 | tf_op jit(solution)/shard_map/the,hed->td/dot_general | solution.py:90
  264.1 1.0 copy-done.9
  265.1 15.1 %fusion.13 = f32[128,8192]{1,0:T(8,128)} fusion(bf16[3,2048,8192]{2,1,0:T(8,128)(2,1)} %param.21, f32[128,2048]{1,0:T(8,128)S(1)} %get-tuple-element.41, f32[2048]{0:T(1024)S(1)} %bitcast.478, f32[128]{0:T(128)S(1)} %add_rsqrt_fusion.2), kind=kOutput, calls=%fused_computation.14 | convolution fusion | flops 4295753728 | bytes 38806016 | tf_op jit(solution)/shard_map/dot_general | solution.py:34
  280.2 29.6 %multiply_reduce_fusion.1 = (f32[128]{0:T(128)S(1)}, f32[128,2048]{1,0:T(8,128)}) fusion(f32[128,2048]{1,0:T(8,128)} %copy-done.9, bf16[3,8192,2048]{2,1,0:T(8,128)(2,1)} %param.23, bf16[3,2048,8192]{2,1,0:T(8,128)(2,1)} %param.22, f32[128,8192]{1,0:T(8,128)} %fusion.13, f32[2048]{0:T(1024)S(1)} %bitcast.479, f32[128]{0:T(128)S(1)} %add_rsqrt_fusion.2), kind=kOutput, calls=%fused_computation.121 | convolution fusion | flops 8598323200 | bytes 74458112 | tf_op jit(solution)/shard_map/dot_general | solution.py:37
  309.8 1.4 multiply_convert_fusion.1
  311.3 0.7 fusion.341
  312.1 0.7 maximum_convert_fusion.2
  312.8 0.2 copy.41
  313.0 0.2 copy.42
  313.2 2.3 fusion.340
  315.6 0.2 copy.43
  315.8 1.7 pad_maximum_fusion.6
  317.5 5.1 %all-to-all-start.1 = ((bf16[3,128,512]{1,0,2:T(4,128)(2,1)}), bf16[3,128,512]{1,0,2:T(4,128)(2,1)S(1)}, u32[]{:S(2)}, u32[]{:S(2)}) async-start(bf16[3,128,512]{1,0,2:T(4,128)(2,1)} %pad_maximum_fusion.6), calls=%async_computation.1 | async-start | bytes 1048576 | tf_op jit(solution)/shard_map/all_to_all | solution.py:95
  322.7 0.2 copy.36
  322.9 0.2 copy.37
  323.1 1.1 copy.38
  324.3 1.7 pad_maximum_fusion.5
  326.0 5.7 %fusion.342 = f32[128,2048]{0,1:S(1)} fusion(bf16[128,2048]{1,0:T(8,128)(2,1)S(1)} %multiply_convert_fusion.1, bf16[2048,2048]{0,1:T(8,128)(2,1)} %bitcast.427), kind=kOutput, calls=%fused_computation.227 | convolution fusion | flops 1073741824 | bytes 9961472
  331.8 10.6 %all-to-all-done.1 = bf16[3,128,512]{1,0,2:T(4,128)(2,1)S(1)} async-done(((bf16[3,128,512]{1,0,2:T(4,128)(2,1)}), bf16[3,128,512]{1,0,2:T(4,128)(2,1)S(1)}, u32[]{:S(2)}, u32[]{:S(2)}) %all-to-all-start.1) | async-done | bytes 393248 | tf_op jit(solution)/shard_map/all_to_all | solution.py:95
  342.4 4.3 all-to-all-start
  346.9 0.3 reshape.190
  347.2 1.7 fusion.316
  349.3 0.3 copy.45
  349.7 1.4 reshape.191
  351.0 11.9 %all-to-all-done = bf16[3,128,512]{1,0,2:T(4,128)(2,1)S(1)} async-done(((bf16[3,128,512]{1,0,2:T(4,128)(2,1)}), bf16[3,128,512]{1,0,2:T(4,128)(2,1)S(1)}, u32[]{:S(2)}, u32[]{:S(2)}) %all-to-all-start) | async-done | bytes 393248 | tf_op jit(solution)/shard_map/all_to_all | solution.py:94
  363.0 0.3 reshape.188
  363.3 1.7 fusion.317
  365.5 0.3 copy.40
  365.8 1.4 reshape.189
  367.1 12.6 %fusion.332 = f32[8,4,128]{2,1,0:T(4,128)S(1)} fusion(pred[128,2048]{0,1:T(8,128)(4,1)S(1)} %compare_and_fusion, bf16[2048,8,64]{0,2,1:T(8,128)(2,1)} %all-gather.19.cloned.1.call-done, bf16[128,8,4,32]{0,3,2,1:T(8,128)(2,1)S(1)} %bitcast.462, bf16[128,8,4,32]{0,3,2,1:T(8,128)(2,1)S(1)} %bitcast.460), kind=kOutput, calls=%fused_computation.221 | convolution fusion | flops 1108346880 | bytes 2899968 | tf_op jit(solution)/shard_map/sub | solution.py:47
  379.8 22.3 %all-gather.17.cloned.1.call-done = bf16[2048,8,64]{0,2,1:T(8,128)(2,1)} async-done(((bf16[128,8,64]{0,2,1:T(8,128)(2,1)}), bf16[2048,8,64]{0,2,1:T(8,128)(2,1)}) %all-gather.17.cloned.1.call-update) | async-done | bytes 2097168 | tf_op jit(solution)/shard_map/all_gather | solution.py:88
  402.1 17.0 %fusion.211 = bf16[8,64,4,128]{3,1,2,0:T(8,128)(2,1)S(1)} fusion(f32[8,4,128]{2,1,0:T(4,128)S(1)} %fusion.332, pred[128,2048]{0,1:T(8,128)(4,1)S(1)} %compare_and_fusion, bf16[2048,8,64]{0,2,1:T(8,128)(2,1)} %all-gather.19.cloned.1.call-done, bf16[2048,8,64]{0,2,1:T(8,128)(2,1)} %all-gather.17.cloned.1.call-done, ...), kind=kOutput, calls=%fused_computation.112 | convolution fusion | flops 2190743552 | bytes 5521408 | tf_op jit(solution)/shard_map/kgts,skd->tkgd/dot_general | solution.py:49
  419.1 4.7 %multiply_reduce_fusion = (f32[128]{0:T(128)S(1)}, f32[128,2048]{1,0:T(8,128)S(1)}) fusion(f32[128,2048]{1,0:T(8,128)S(1)} %copy-done.2, bf16[128,32,64]{0,2,1:T(8,128)(2,1)S(1)} %bitcast.455, bf16[3,32,64,2048]{3,2,1,0:T(8,128)(2,1)} %param.20), kind=kOutput, calls=%fused_computation.119 | convolution fusion | flops 1075052416 | bytes 11010560 | tf_op jit(solution)/shard_map/the,hed->td/dot_general | solution.py:90
  423.9 15.1 %fusion.7 = f32[128,8192]{1,0:T(8,128)} fusion(bf16[3,2048,8192]{2,1,0:T(8,128)(2,1)} %param.21, f32[128,2048]{1,0:T(8,128)S(1)} %get-tuple-element.45, f32[2048]{0:T(1024)S(1)} %bitcast.476, f32[128]{0:T(128)S(1)} %add_rsqrt_fusion), kind=kOutput, calls=%fused_computation.7 | convolution fusion | flops 4295753728 | bytes 38806016 | tf_op jit(solution)/shard_map/dot_general | solution.py:34
  439.0 25.4 %fusion.147 = bf16[128,2048]{1,0:T(8,128)(2,1)} fusion(f32[128,2048]{1,0:T(8,128)S(1)} %get-tuple-element.45, bf16[3,8192,2048]{2,1,0:T(8,128)(2,1)} %param.23, bf16[3,2048,8192]{2,1,0:T(8,128)(2,1)} %param.22, f32[128,8192]{1,0:T(8,128)} %fusion.7, f32[2048]{0:T(1024)S(1)} %bitcast.477, f32[128]{0:T(128)S(1)} %add_rsqrt_fusion), kind=kOutput, calls=%fused_computation.87 | convolution fusion | flops 8597536768 | bytes 73933312 | tf_op jit(solution)/shard_map/dot_general | solution.py:37
  (70 shorter events, 2.6 us)
Async XLA Ops:
  7.2 6.7 %copy-start = (bf16[128,2048]{1,0:T(8,128)(2,1)S(1)}, bf16[128,2048]{1,0:T(8,128)(2,1)}, u32[]{:S(2)}) copy-start(bf16[128,2048]{1,0:T(8,128)(2,1)} %param.12) | copy-start | bytes 1572868
  7.2 6.9 %copy-start.14 = (s32[128]{0:T(128)S(1)}, s32[128]{0:T(128)}, u32[]{:S(2)}) copy-start(s32[128]{0:T(128)} %param.13) | copy-start | bytes 1540
  7.2 73.5 %all-gather.11.cloned.1.call-start = ((), (), s32[]{:S(2)}) async-start(), calls=%async_computation.3 | async-start | bytes 2228224 | tf_op jit(solution)/shard_map/all_gather | solution.py:87
  15.8 80.9 %all-gather.9.cloned.1.call-start = ((), (), s32[]{:S(2)}) async-start(), calls=%async_computation.2 | async-start | bytes 2228224 | tf_op jit(solution)/shard_map/all_gather | solution.py:88
  23.5 14.8 %copy-start.15 = (s32[128]{0:T(128)S(1)}, s32[128]{0:T(128)}, u32[]{:S(2)}) copy-start(s32[128]{0:T(128)} %param.14) | copy-start | bytes 1540
  23.5 181.0 %all-gather.15.cloned.1.call-start = ((), (), s32[]{:S(2)}) async-start(), calls=%async_computation.5 | async-start | bytes 2228224 | tf_op jit(solution)/shard_map/all_gather | solution.py:87
  76.1 2.6 copy-start.10
  168.1 74.0 %all-gather.13.cloned.1.call-start = ((), (), s32[]{:S(2)}) async-start(), calls=%async_computation.4 | async-start | bytes 2228224 | tf_op jit(solution)/shard_map/all_gather | solution.py:88
  171.3 195.9 %all-gather.19.cloned.1.call-start = ((), (), s32[]{:S(2)}) async-start(), calls=%async_computation.7 | async-start | bytes 2228224 | tf_op jit(solution)/shard_map/all_gather | solution.py:87
  217.1 42.2 %copy-start.3 = (f32[128,2048]{1,0:T(8,128)S(1)}, f32[128,2048]{1,0:T(8,128)}, u32[]{:S(2)}) copy-start(f32[128,2048]{1,0:T(8,128)} %get-tuple-element.39) | copy-start | bytes 3145732
  259.3 5.8 %copy-start.13 = (f32[1,2048]{1,0:T(1,128)S(1)}, f32[1,2048]{1,0:T(1,128)}, u32[]{:S(2)}) copy-start(f32[1,2048]{1,0:T(1,128)} %get-tuple-element.30) | copy-start | bytes 24580
  264.1 1.0 copy-start.9
  280.2 29.6 %copy-start.11 = (f32[1,2048]{1,0:T(1,128)S(1)}, f32[1,2048]{1,0:T(1,128)}, u32[]{:S(2)}) copy-start(f32[1,2048]{1,0:T(1,128)} %get-tuple-element.31) | copy-start | bytes 24580
  280.2 31.1 %copy-start.1 = (bf16[1,2048,8,64]{1,3,2,0:T(8,128)(2,1)S(1)}, bf16[1,2048,8,64]{1,3,2,0:T(8,128)(2,1)}, u32[]{:S(2)}) copy-start(bf16[1,2048,8,64]{1,3,2,0:T(8,128)(2,1)} %get-tuple-element.9) | copy-start | bytes 6291460
  280.2 32.6 %copy-start.4 = (bf16[128,8,64]{0,2,1:T(8,128)(2,1)S(1)}, bf16[128,8,64]{0,2,1:T(8,128)(2,1)}, u32[]{:S(2)}) copy-start(bf16[128,8,64]{0,2,1:T(8,128)(2,1)} %convert_element_type.167) | copy-start | bytes 393220
  280.2 32.8 %copy-start.6 = (bf16[128,8,64]{0,2,1:T(8,128)(2,1)S(1)}, bf16[128,8,64]{0,2,1:T(8,128)(2,1)}, u32[]{:S(2)}) copy-start(bf16[128,8,64]{0,2,1:T(8,128)(2,1)} %convert_element_type.180) | copy-start | bytes 393220
  309.8 12.9 %copy-start.7 = (bf16[128,8,64]{0,2,1:T(8,128)(2,1)S(1)}, bf16[128,8,64]{0,2,1:T(8,128)(2,1)}, u32[]{:S(2)}) copy-start(bf16[128,8,64]{0,2,1:T(8,128)(2,1)} %maximum_convert_fusion) | copy-start | bytes 393220
  309.8 13.1 %copy-start.8 = (bf16[128,8,64]{0,2,1:T(8,128)(2,1)S(1)}, bf16[128,8,64]{0,2,1:T(8,128)(2,1)}, u32[]{:S(2)}) copy-start(bf16[128,8,64]{0,2,1:T(8,128)(2,1)} %maximum_convert_fusion.1) | copy-start | bytes 393220
  315.6 8.7 %copy-start.5 = (bf16[128,8,64]{0,2,1:T(8,128)(2,1)}, bf16[128,8,64]{0,2,1:T(8,128)(2,1)S(1)}, u32[]{:S(2)}) copy-start(bf16[128,8,64]{0,2,1:T(8,128)(2,1)S(1)} %convert_element_type.192) | copy-start | bytes 393220
  317.5 24.9 %all-to-all-start.1 = ((bf16[3,128,512]{1,0,2:T(4,128)(2,1)}), bf16[3,128,512]{1,0,2:T(4,128)(2,1)S(1)}, u32[]{:S(2)}, u32[]{:S(2)}) async-start(bf16[3,128,512]{1,0,2:T(4,128)(2,1)} %pad_maximum_fusion.6), calls=%async_computation.1 | async-start | bytes 1048576 | tf_op jit(solution)/shard_map/all_to_all | solution.py:95
  322.6 79.5 %all-gather.17.cloned.1.call-start = ((), (), s32[]{:S(2)}) async-start(), calls=%async_computation.6 | async-start | bytes 2228224 | tf_op jit(solution)/shard_map/all_gather | solution.py:88
  342.4 20.6 %all-to-all-start = ((bf16[3,128,512]{1,0,2:T(4,128)(2,1)}), bf16[3,128,512]{1,0,2:T(4,128)(2,1)S(1)}, u32[]{:S(2)}, u32[]{:S(2)}) async-start(bf16[3,128,512]{1,0,2:T(4,128)(2,1)} %pad_maximum_fusion.5), calls=%async_computation | async-start | bytes 1048576 | tf_op jit(solution)/shard_map/all_to_all | solution.py:94
  379.8 39.3 %copy-start.2 = (f32[128,2048]{1,0:T(8,128)S(1)}, f32[128,2048]{1,0:T(8,128)}, u32[]{:S(2)}) copy-start(f32[128,2048]{1,0:T(8,128)} %get-tuple-element.43) | copy-start | bytes 3145732
  419.1 4.8 %copy-start.12 = (f32[1,2048]{1,0:T(1,128)S(1)}, f32[1,2048]{1,0:T(1,128)}, u32[]{:S(2)}) copy-start(f32[1,2048]{1,0:T(1,128)} %get-tuple-element.28) | copy-start | bytes 24580
Sparse Core Ops, SparseCore 0:
  15.9 42.3 all-gather.10
  60.4 36.2 all-gather.8
  168.3 36.2 all-gather.14
  205.9 36.2 all-gather.12
  312.9 50.8 all-gather.18
  365.2 36.8 all-gather.16
where the time goes:
time: 476 us; the launch traced here: 472 us
  matrix products  257 us (54%)
  waiting for transfers between devices  101 us (21%)
  blocking collectives  37.8 us (8%)
  local copies, waits for them, and re-layouts  37.1 us (8%)
  between operations  15.1 us (3%)
  other arithmetic  14.2 us (3%)
  starting transfers between devices  9.8 us (2%)
    dot_general x3, matrix products, mlp_block(): jnp.dot(gated_act, w_down, preferred_element_type=jnp.float32)  84.7 us
    dot_general x3, matrix products, local_attention(): jnp.einsum('kgts,skd->tkgd', attn_prob, v_full, preferred_element_type=jn...  51.7 us
    all_gather x3, waiting for transfers between devices, local_step(): v_full = lax.all_gather(v_new, 'cp', tiled=True)  50.7 us
    dot_general x3, matrix products, mlp_block(): gate_pre = jnp.dot(normed, w_up1, preferred_element_type=jnp.float32)  45.6 us
    sub x3, matrix products, local_attention(): exp_scores = jnp.exp(scores - row_max)  37.9 us
    all_gather x3, waiting for transfers between devices, local_step(): k_full = lax.all_gather(k_rot, 'cp', tiled=True)  27.3 us
    all_gather x1, blocking collectives, local_step(): all_seg = lax.all_gather(segments, 'cp', tiled=True)  22.7 us
    unnamed x9, matrix products  21.6 us
  transfers between devices with their start and end apart: 8, of which 6 were waited for; matrix products, arithmetic and copies ran while one was open for 20% of the time, Pallas kernels for 0%

commit v1 on v0

v1 whole, which is shorter than its diff:
```python
import functools
import math

import jax
import jax.numpy as jnp
from jax import lax
from jax.experimental import pallas as pl
from jax.experimental.pallas import tpu as pltpu
from jax.sharding import PartitionSpec as P

NORM_EPS = 1e-5
ROPE_THETA = 10000.0
MASK_FILL = -1e30
BIG = 3e38
LOG2E = math.log2(math.e)
MESH = pl.DeviceIdType.MESH
F32 = jnp.float32
BF16 = jnp.bfloat16
NT = (((1,), (1,)), ((), ()))
NA = 8
UP, DN, D2D = 0, 1, 2


def kernel(cfg, x_in, pos_in, cos_in, sin_in, g1_in, g2_in, wq, wk, wv, wo, w1, w3, w2,
           x_out, kc, vc,
           ring_a, ring_b, kv, knat, qx, oacc, m_st, l_st, cap, xs, hs, ub, acc,
           sem_a, sem_b, send_sem, recv_sem, cred, csem):
    n_layers, n_cp, nb = cfg["layers"], cfg["n_cp"], cfg["nb"]
    n_tok, d_model = xs.shape
    n_chip = n_cp // 2
    n_kv = oacc.shape[0]
    head_dim = oacc.shape[1]
    lanes = oacc.shape[2]
    q_group = lanes // n_tok
    kvw = n_kv * head_dim
    half = head_dim // 2
    rows_a = ring_a.shape[1]
    cols_b = ring_b.shape[2]
    n_ff = w1.shape[2] // cols_b
    n_q = wq.shape[1] // rows_a
    n_o = wo.shape[1] // rows_a
    n_pos = 2 + n_q + n_o + n_ff
    first_q, first_o, first_w2 = 2, 2 + n_q, 2 + n_q + n_o

    me = lax.axis_index("cp")
    z, c = me // 2, me % 2
    up = ((z + 1) % n_chip) * 2 + c
    dn = ((z + n_chip - 1) % n_chip) * 2 + c
    partner = z * 2 + (1 - c)

    def a_copy(l, pos):
        slot = lax.rem(l * n_pos + pos, NA)
        if isinstance(pos, int):
            if pos == 0:
                src = wk.at[l]
            elif pos == 1:
                src = wv.at[l]
            elif pos < first_o:
                src = wq.at[l, pl.ds((pos - first_q) * rows_a, rows_a), :]
            elif pos < first_w2:
                src = wo.at[l, pl.ds((pos - first_o) * rows_a, rows_a), :]
            else:
                src = w2.at[l, pl.ds((pos - first_w2) * rows_a, rows_a), :]
        else:
            src = w2.at[l, pl.ds(pl.multiple_of((pos - first_w2) * rows_a, rows_a), rows_a), :]
        return pltpu.make_async_copy(src, ring_a.at[slot], sem_a.at[slot])

    def a_slot(l, pos):
        return lax.rem(l * n_pos + pos, NA)

    def b_copy(l, j, t):
        w = w1 if t == 0 else w3
        slot = lax.rem((l * n_ff + j) * 2 + t, nb)
        src = w.at[l, :, pl.ds(pl.multiple_of(j * cols_b, cols_b), cols_b)]
        return pltpu.make_async_copy(src, ring_b.at[slot], sem_b.at[slot])

    def ring_copy(dirn, tile, part):
        ref = kv.at[tile, pl.ds(part * kvw, kvw), :]
        dev = (up, dn, partner)[dirn]
        return pltpu.make_async_remote_copy(
            src_ref=ref, dst_ref=ref, send_sem=send_sem.at[dirn, tile, part],
            recv_sem=recv_sem.at[tile, part], device_id={"cp": dev}, device_id_type=MESH)

    for pos in range(NA):
        a_copy(0, pos).start()
    for j in range(nb // 2):
        for t in range(2):
            b_copy(0, j, t).start()

    barrier = pltpu.get_barrier_semaphore()
    for dev in (up, dn, partner):
        pl.semaphore_signal(barrier, inc=1, device_id={"cp": dev}, device_id_type=MESH)

    xs[...] = x_in[...]
    qx[...] = jnp.zeros_like(qx)
    pl.semaphore_wait(barrier, 3)

    half_tok = n_tok // 2

    def norm_rows(gain):
        blk = 16

        def one(r, carry):
            rows = pl.ds(pl.multiple_of(r * blk, blk), blk)
            v = xs[rows, :].astype(F32)
            inv = lax.rsqrt(jnp.mean(v * v, axis=-1, keepdims=True) + NORM_EPS)
            hs[rows, :] = (v * inv * gain).astype(BF16)
            return carry

        lax.fori_loop(0, n_tok // blk, one, 0, unroll=2)

    def resid_rows():
        blk = 16

        def one(r, carry):
            rows = pl.ds(pl.multiple_of(r * blk, blk), blk)
            xs[rows, :] = (xs[rows, :].astype(F32) + acc[rows, :]).astype(BF16)
            return carry

        lax.fori_loop(0, n_tok // blk, one, 0, unroll=2)

    def rope_t(t):
        nh = t.shape[0] // head_dim
        cos_b = cos_in[...]
        sin_b = sin_in[...]
        outs = []
        for n in range(nh):
            a = t[n * head_dim:n * head_dim + half]
            b = t[n * head_dim + half:(n + 1) * head_dim]
            outs.append(a * cos_b - b * sin_b)
            outs.append(b * cos_b + a * sin_b)
        return outs

    lane = lax.broadcasted_iota(jnp.int32, (1, n_tok), 1)
    n_blk = 2 * n_cp

    def nat_of(tile, idx):
        return jnp.where(idx < half_tok, tile * half_tok + idx, (n_blk - 1 - tile) * half_tok + idx - half_tok)

    def attend(chip):
        nat_q = nat_of(me, lane)
        start_q = nat_q - pos_in[...]
        for s in range(2):
            key = lax.broadcasted_iota(jnp.int32, (n_tok, n_tok), 0)
            nat_k = nat_of(chip * 2 + s, key)
            ok = (nat_k >= start_q) & (nat_k <= nat_q)
            cap[s * n_tok:(s + 1) * n_tok, :] = jnp.where(ok, BIG, MASK_FILL)
            for p in range(n_kv // 2):
                kt = kv[chip * 2 + s, p * 2 * head_dim:(p + 1) * 2 * head_dim, :]
                knat[p, s * n_tok:(s + 1) * n_tok, :] = kt.T

        def one_g(i, carry):
            for gg in range(4):
                g = i * 4 + gg
                k_blk = knat[i * 2 + gg // 2]
                rows = pl.ds(pl.multiple_of(kvw + g * head_dim, head_dim), head_dim)
                v_blk = jnp.concatenate([kv[chip * 2, rows, :], kv[chip * 2 + 1, rows, :]], axis=1)
                m_row = m_st[g]
                l_row = l_st[g]
                for hf in range(q_group // 2):
                    ls = slice(hf * 2 * n_tok, (hf + 1) * 2 * n_tok)
                    s_t = jnp.dot(k_blk, qx[g, :, ls], preferred_element_type=F32)
                    cap2 = jnp.concatenate([cap[...], cap[...]], axis=1)
                    s_t = jnp.minimum(s_t, cap2) * LOG2E
                    m_old = m_row[0:1, ls]
                    m_new = jnp.maximum(m_old, jnp.max(s_t, axis=0, keepdims=True))
                    e = jnp.exp2(s_t - m_new)
                    alpha = jnp.exp2(m_old - m_new)
                    m_st[g, 0:1, ls] = m_new
                    l_st[g, 0:1, ls] = l_row[0:1, ls] * alpha + jnp.sum(e, axis=0, keepdims=True)
                    pv = jnp.dot(v_blk, e.astype(BF16), preferred_element_type=F32)
                    oacc[g, :, ls] = oacc[g, :, ls] * alpha + pv
            return carry

        lax.fori_loop(0, n_kv // 4, one_g, 0)

    def tile_of(dist):
        return lax.rem(z + dist + n_chip, n_chip) * 2 + c

    far = n_chip // 2

    def layer(l, carry):
        has_next = l + 1 < n_layers

        norm_rows(g1_in[l])

        @pl.when(l > 0)
        def _():
            for i in range(3):
                pl.semaphore_wait(cred.at[i], 1)

        for part in range(2):
            a_copy(l, part).wait()
            t = lax.dot_general(ring_a[a_slot(l, part)], hs[...], NT, preferred_element_type=F32)
            if part == 0:
                for n, blk in enumerate(rope_t(t)):
                    kv[me, n * half:(n + 1) * half, :] = blk.astype(BF16)
            else:
                kv[me, kvw:2 * kvw, :] = t.astype(BF16)
            for dirn in (UP, DN, D2D):
                ring_copy(dirn, me, part).start()
            a_copy(l, part + NA).start()

        for i in range(n_q):
            pos = first_q + i
            a_copy(l, pos).wait()
            t = lax.dot_general(ring_a[a_slot(l, pos)], hs[...], NT, preferred_element_type=F32)
            for n, blk in enumerate(rope_t(t)):
                head = i * (rows_a // head_dim) + n // 2
                g, slot = head // q_group, head % q_group
                r0 = (g % 2) * head_dim + (n % 2) * half
                qx[g, r0:r0 + half, slot * n_tok:(slot + 1) * n_tok] = (blk.astype(BF16).astype(F32) * head_dim ** -0.5).astype(BF16)
            a_copy(l, pos + NA).start()

        m_st[...] = jnp.full_like(m_st, MASK_FILL * LOG2E)
        l_st[...] = jnp.zeros_like(l_st)
        oacc[...] = jnp.zeros_like(oacc)

        def step(k, carry):
            dist = (k + 1) // 2

            def serve(part):
                lo, hi = tile_of(-dist), tile_of(dist)

                @pl.when(dist < far)
                def _():
                    ring_copy(UP, lo, part).wait_recv()

                    @pl.when((dist < far - 1) | (part == 0))
                    def _():
                        ring_copy(UP, lo, part).start()

                    ring_copy(D2D, lo, part).start()
                    ring_copy(DN, hi, part).wait_recv()

                    @pl.when((dist < far - 1) | (part == 1))
                    def _():
                        ring_copy(DN, hi, part).start()

                    ring_copy(D2D, hi, part).start()

                @pl.when(dist == far)
                def _():
                    ring_copy(UP, lo, part).wait_recv()
                    ring_copy(D2D, lo, part).start()

            @pl.when(k % 2 == 1)
            def _():
                serve(0)
                serve(1)

            chip = jnp.where(k % 2 == 1, z - dist + n_chip, z + dist) % n_chip
            other = chip * 2 + 1 - c
            for part in range(2):
                ring_copy(D2D, other, part).wait_recv()
            attend(chip)
            return carry

        lax.fori_loop(0, n_chip, step, 0)

        r0 = pl.multiple_of(me * (kvw // n_cp), kvw // n_cp)
        ck = pltpu.make_async_copy(kv.at[:, pl.ds(r0, kvw // n_cp), :], kc.at[l], csem.at[0])
        cv = pltpu.make_async_copy(kv.at[:, pl.ds(kvw + r0, kvw // n_cp), :], vc.at[l], csem.at[1])
        ck.start()
        cv.start()

        for i in range(n_o):
            pos = first_o + i
            a_copy(l, pos).wait()
            n_g = rows_a // (q_group * head_dim)
            parts = []
            for gg in range(n_g):
                g = i * n_g + gg
                o = oacc[g] * (1.0 / l_st[g, 0:1, :])
                for hh in range(q_group):
                    parts.append(o[:, hh * n_tok:(hh + 1) * n_tok])
            o_t = jnp.concatenate(parts, axis=0)
            o_n = o_t.T.astype(BF16)
            y = jnp.dot(o_n, ring_a[a_slot(l, pos)], preferred_element_type=F32)
            if i == 0:
                acc[...] = y
            else:
                acc[...] += y
            a_copy(l, pos + NA).start()
        resid_rows()

        ck.wait()
        cv.wait()
        for part in range(2):
            for dirn in (UP, DN, D2D):
                ring_copy(dirn, me, part).wait_send()
            for dist in range(1, far):
                lo, hi = tile_of(-dist), tile_of(dist)
                if dist < far - 1 or part == 0:
                    ring_copy(UP, lo, part).wait_send()
                if dist < far - 1 or part == 1:
                    ring_copy(DN, hi, part).wait_send()
                ring_copy(D2D, lo, part).wait_send()
                ring_copy(D2D, hi, part).wait_send()
            ring_copy(D2D, tile_of(far), part).wait_send()

        @pl.when(has_next)
        def _():
            pl.semaphore_signal(cred.at[DN], inc=1, device_id={"cp": up}, device_id_type=MESH)
            pl.semaphore_signal(cred.at[UP], inc=1, device_id={"cp": dn}, device_id_type=MESH)
            pl.semaphore_signal(cred.at[D2D], inc=1, device_id={"cp": partner}, device_id_type=MESH)

        norm_rows(g2_in[l])

        def up_part(j):
            for t in range(2):
                b_copy(l, j, t).wait()
            s0 = lax.rem((l * n_ff + j) * 2, nb)
            a = jnp.dot(hs[...], ring_b[s0], preferred_element_type=F32)
            b = jnp.dot(hs[...], ring_b[s0 + 1], preferred_element_type=F32)
            ub[lax.rem(j, 2)] = (jax.nn.silu(a) * b).astype(BF16)

        def up_refill(j):
            j2 = j + nb // 2
            l2 = l + j2 // n_ff

            @pl.when(l2 < n_layers)
            def _():
                for t in range(2):
                    b_copy(l2, lax.rem(j2, n_ff), t).start()

        def down_refill(j):
            @pl.when(j + NA < n_ff)
            def _():
                a_copy(l, first_w2 + j + NA).start()

            for pos in range(NA):
                @pl.when((j + NA - n_ff == pos) & has_next)
                def _():
                    a_copy(l + 1, pos).start()

        def mlp(j, carry):
            a_copy(l, first_w2 + j - 1).wait()
            up_part(j)
            acc[...] += jnp.dot(ub[lax.rem(j - 1, 2)], ring_a[a_slot(l, first_w2 + j - 1)], preferred_element_type=F32)
            up_refill(j)
            down_refill(j - 1)
            return carry

        acc[...] = jnp.zeros_like(acc)
        up_part(0)
        up_refill(0)
        lax.fori_loop(1, n_ff, mlp, 0)
        a_copy(l, first_w2 + n_ff - 1).wait()
        acc[...] += jnp.dot(ub[(n_ff - 1) % 2], ring_a[a_slot(l, first_w2 + n_ff - 1)], preferred_element_type=F32)
        down_refill(n_ff - 1)
        resid_rows()
        return carry

    lax.fori_loop(0, n_layers, layer, 0)
    x_out[...] = xs[...]


def to_natural(cache):
    n_layers, n_dev, n_cols, n_tok = cache.shape
    blocks = cache.reshape(n_layers, n_dev, n_cols, 2, n_tok // 2)
    front = blocks[:, :, :, 0]
    back = jnp.flip(blocks[:, :, :, 1], axis=1)
    both = jnp.concatenate([front, back], axis=1)
    both = jnp.transpose(both, (0, 2, 1, 3)).reshape(n_layers, n_cols, n_dev * n_tok)
    return jnp.transpose(both, (0, 2, 1))


def solution(mesh):
    n_cp = mesh.shape["cp"]
    row_spec = P(("req", "cp"), None)
    tok_spec = P(("req", "cp"))
    rep_spec = P()
    cache_spec = P(None, "req", "cp")

    def local_step(hidden, positions, segments, gain_1, gain_2, w_q, w_k, w_v, w_o, w_1, w_3, w_2):
        n_layers, d_model, n_heads, head_dim = w_q.shape
        n_kv = w_k.shape[2]
        n_tok = hidden.shape[0]
        kvw = n_kv * head_dim
        q_group = n_heads // n_kv
        rows_a, cols_b, nb = kvw, 512, 16
        inv_freq = ROPE_THETA ** (-2.0 * jnp.arange(head_dim // 2, dtype=F32) / head_dim)
        angle = inv_freq[:, None] * positions.astype(F32)[None, :]
        cos_t, sin_t = jnp.cos(angle), jnp.sin(angle)

        def turned(w):
            return jnp.transpose(w, (0, 2, 3, 1)).reshape(n_layers, -1, d_model)

        cfg = dict(layers=n_layers, n_cp=n_cp, nb=nb)
        vmem = pl.BlockSpec(memory_space=pltpu.VMEM)
        hbm = pl.BlockSpec(memory_space=pl.ANY)
        cache = jax.ShapeDtypeStruct((n_layers, n_cp, kvw // n_cp, n_tok), BF16)
        x, k_c, v_c = pl.pallas_call(
            functools.partial(kernel, cfg),
            out_shape=(jax.ShapeDtypeStruct(hidden.shape, BF16), cache, cache),
            in_specs=[vmem] * 6 + [hbm] * 7,
            out_specs=(vmem, hbm, hbm),
            scratch_shapes=[
                pltpu.VMEM((NA, rows_a, d_model), BF16),
                pltpu.VMEM((nb, d_model, cols_b), BF16),
                pltpu.VMEM((n_cp, 2 * kvw, n_tok), BF16),
                pltpu.VMEM((n_kv // 2, 2 * n_tok, 2 * head_dim), BF16),
                pltpu.VMEM((n_kv, 2 * head_dim, q_group * n_tok), BF16),
                pltpu.VMEM((n_kv, head_dim, q_group * n_tok), F32),
                pltpu.VMEM((n_kv, 8, q_group * n_tok), F32),
                pltpu.VMEM((n_kv, 8, q_group * n_tok), F32),
                pltpu.VMEM((2 * n_tok, n_tok), F32),
                pltpu.VMEM((n_tok, d_model), BF16),
                pltpu.VMEM((n_tok, d_model), BF16),
                pltpu.VMEM((2, n_tok, cols_b), BF16),
                pltpu.VMEM((n_tok, d_model), F32),
                pltpu.SemaphoreType.DMA((NA,)),
                pltpu.SemaphoreType.DMA((nb,)),
                pltpu.SemaphoreType.DMA((3, n_cp, 2)),
                pltpu.SemaphoreType.DMA((n_cp, 2)),
                pltpu.SemaphoreType.REGULAR((3,)),
                pltpu.SemaphoreType.DMA((2,)),
            ],
            compiler_params=pltpu.CompilerParams(
                collective_id=0, has_side_effects=True, vmem_limit_bytes=67043328),
            name="prefill",
        )(
            hidden, positions[None, :], cos_t, sin_t,
            gain_1.astype(F32)[:, None, :], gain_2.astype(F32)[:, None, :],
            turned(w_q), turned(w_k), turned(w_v), w_o.reshape(n_layers, -1, d_model), w_1, w_3, w_2,
        )
        return x, to_natural(k_c), to_natural(v_c)

    return jax.shard_map(
        local_step,
        mesh=mesh,
        in_specs=(row_spec, tok_spec, tok_spec) + (rep_spec,) * 9,
        out_specs=(row_spec, cache_spec, cache_spec),
        check_vma=False,
    )
```

time: 476 us -> 254 us (0.53)
  matrix products: 257 us -> 0 us
  Pallas kernels: 0 us -> 235 us
  waiting for transfers between devices: 101 us -> 0 us
  blocking collectives: 37.8 us -> 0 us
  local copies, waits for them, and re-layouts: 37.1 us -> 16.3 us
  between operations: 15.1 us -> 0.73 us
  other arithmetic: 14.2 us -> 1.74 us
  starting transfers between devices: 9.8 us -> 0 us
    pallas_call x0 -> x1, Pallas kernels: none -> 235 us  [local_step(): pl.pallas_call(functools.partial(kernel, cfg), out_shape=(jax.ShapeDtypeS...]
    dot_general x12 -> x0, matrix products: 197 us -> none  [the longest x3 84.7 us: mlp_block(): jnp.dot(gated_act, w_down, preferred_element_type=jnp.float32)]
    all_gather x6 -> x0, waiting for transfers between devices: 78 us -> none  [the longest x3 50.7 us: local_step(): v_full = lax.all_gather(v_new, 'cp', tiled=True)]
    sub x3 -> x0, matrix products: 37.9 us -> none  [local_attention(): exp_scores = jnp.exp(scores - row_max)]
    all_gather x2 -> x0, blocking collectives: 37.8 us -> none  [the longest x1 22.7 us: local_step(): all_seg = lax.all_gather(segments, 'cp', tiled=True)]
    slice x5 -> x2, local copies, waits for them, and re-layouts: 29.4 us -> 3.49 us  [to_natural(): front = blocks[:, :, :, 0]]
    all_to_all x2 -> x0, waiting for transfers between devices: 22.5 us -> none  [the longest x1 11.9 us: local_step(): k_cache = lax.all_to_all(jnp.stack(k_keep), 'cp', 2, 1, tiled=True)]
    unnamed x9 -> x0, matrix products: 21.6 us -> none
  transfers between devices with their start and end apart: 8 -> 0, of which waited for: 6 -> 0; matrix products, arithmetic and copies ran while one was open for 20% -> 0% of each run, Pallas kernels for 0% -> 0%
where the time goes in v1:
time: 254 us
  Pallas kernels  235 us (93%)
  local copies, waits for them, and re-layouts  16.3 us (6%)
    pallas_call x1, Pallas kernels, local_step(): pl.pallas_call(functools.partial(kernel, cfg), out_shape=(jax.ShapeDtypeS...  235 us

profile of v1, /device:TPU:21, one launch (start us, length us, event | category | flops | bytes accessed | tf_op | source)
XLA Modules:
  0.0 253.6 jit_solution(1704014108228773243)
XLA Ops:
  0.6 0.7 convert_element_type.2
  1.3 0.8 multiply_sine_fusion
  2.1 1.3 reshape.44.g1_in
  3.4 1.3 reshape.45.g2_in
  4.7 234.9 %prefill.1 = (bf16[128,2048]{1,0:T(8,128)(2,1)}, bf16[3,16,32,128]{3,2,1,0:T(8,128)(2,1)}, bf16[3,16,32,128]{3,2,1,0:T(8,128)(2,1)}) custom-call(bf16[128,2048]{1,0:T(8,128)(2,1)} %x_in.1, s32[1,128]{1,0:T(1,128)} %bitcast.39, f32[32,128]{1,0:T(8,128)} %get-tuple-element.14.cos_in, f32[32,128]{1,0:T(8,128)} %get-tuple-element.13.sin_in, ...), custom_call_target="tpu_custom_call" | custom-call | tf_op jit(solution)/shard_map/prefill/pallas_call | solution.py:394
  239.7 2.3 reshape.42
  242.0 1.7 fusion
  243.7 0.2 copy_bitcast_fusion
  243.9 0.2 maximum_bitcast_fusion.1
  244.1 0.3 copy.27
  244.4 1.4 reshape.43
  245.8 2.1 reshape.40
  248.0 1.7 fusion.1
  249.7 0.2 copy_bitcast_fusion.2
  249.9 0.2 maximum_bitcast_fusion
  250.1 0.3 copy.24
  250.4 1.4 reshape.41
  251.8 1.9 copy.37
  (3 shorter events, 0.1 us)

commit v2 on v1

v2 whole, which is shorter than its diff:
```python
import functools
import math

import jax
import jax.numpy as jnp
from jax import lax
from jax.experimental import pallas as pl
from jax.experimental.pallas import tpu as pltpu
from jax.sharding import PartitionSpec as P

NORM_EPS = 1e-5
ROPE_THETA = 10000.0
MASK_FILL = -1e30
BIG = 3e38
LOG2E = math.log2(math.e)
MESH = pl.DeviceIdType.MESH
F32 = jnp.float32
BF16 = jnp.bfloat16
NT = (((1,), (1,)), ((), ()))
NA = 4
NB = 16
AHEAD = 2
UP, DN, D2D = 0, 1, 2


def kernel(cfg, x_in, pos_in, cos_in, sin_in, g1_in, g2_in, wq, wk, wv, wo, w1, w3, w2,
           x_out, kc, vc,
           ring_a, ring_b, kv, kvt, knat, qx, oacc, m_st, l_st, cap, cbuf, xs, h2, ub, acc, psend, precv, gains,
           sem_a, sem_b, send_sem, recv_sem, hs_sem, hr_sem, ps_sem, pr_sem, cred, csem):
    n_layers, n_cp, nb = cfg["layers"], cfg["n_cp"], cfg["nb"]
    n_tok, d_model = xs.shape
    half_tok = n_tok // 2
    n_chip = n_cp // 2
    n_kv, head_dim, lanes = oacc.shape
    q_group = lanes // n_tok
    lane_f = lanes // 2
    kvw = n_kv * head_dim
    half = head_dim // 2
    rows_a = ring_a.shape[1]
    k_b, cols_b = ring_b.shape[1:]
    own_ff = ub.shape[1]
    n_up = own_ff // cols_b
    n_dn = d_model // cols_b
    n_kh = own_ff // k_b
    n_pair = n_up + n_dn
    ahead_b = nb // 2
    n_q = wq.shape[1] // rows_a
    n_o = wo.shape[1] // rows_a
    n_pos = 2 + n_q + n_o
    first_q, first_o = 2, 2 + n_q
    n_col = kvw // n_cp

    me = lax.axis_index("cp")
    z, c = me // 2, me % 2
    up = ((z + 1) % n_chip) * 2 + c
    dn = ((z + n_chip - 1) % n_chip) * 2 + c
    partner = z * 2 + (1 - c)

    def a_slot(l, pos):
        return lax.rem(l * n_pos + pos, NA)

    def a_copy(l, pos):
        if pos >= n_pos:
            l, pos = l + 1, pos - n_pos
        slot = a_slot(l, pos)
        if pos == 0:
            src = wk.at[l]
        elif pos == 1:
            src = wv.at[l]
        elif pos < first_o:
            src = wq.at[l, pl.ds((pos - first_q) * rows_a, rows_a), :]
        else:
            src = wo.at[l, pl.ds((pos - first_o) * rows_a, rows_a), :]
        return pltpu.make_async_copy(src, ring_a.at[slot], sem_a.at[slot])

    def a_refill(l, pos):
        if pos + NA < n_pos:
            a_copy(l, pos + NA).start()
        else:
            @pl.when(l + 1 < n_layers)
            def _():
                a_copy(l, pos + NA).start()

    def b_slot(l, q, t):
        return lax.rem((l * n_pair + q) * 2 + t, nb)

    def up_copy(l, j, t):
        slot = b_slot(l, j, t)
        col = pl.multiple_of(c * own_ff + j * cols_b, cols_b)
        return pltpu.make_async_copy((w1, w3)[t].at[l, :, pl.ds(col, cols_b)], ring_b.at[slot], sem_b.at[slot])

    def dn_copy(l, n, t):
        slot = b_slot(l, n_up + n, t)
        row = pl.multiple_of(c * own_ff + t * k_b, k_b)
        col = pl.multiple_of(n * cols_b, cols_b)
        return pltpu.make_async_copy(w2.at[l, pl.ds(row, k_b), pl.ds(col, cols_b)], ring_b.at[slot], sem_b.at[slot])

    def b_refill(l, q):
        q2 = q + ahead_b
        l2 = l + q2 // n_pair
        q3 = lax.rem(q2, n_pair)

        @pl.when((l2 < n_layers) & (q3 < n_up))
        def _():
            for t in range(2):
                up_copy(l2, q3, t).start()

        @pl.when((l2 < n_layers) & (q3 >= n_up))
        def _():
            for t in range(2):
                dn_copy(l2, q3 - n_up, t).start()

    def ring_copy(dirn, tile, part):
        ref = kv.at[tile, pl.ds(part * kvw, kvw), :]
        dev = (up, dn, partner)[dirn]
        return pltpu.make_async_remote_copy(
            src_ref=ref, dst_ref=ref, send_sem=send_sem.at[dirn, tile, part],
            recv_sem=recv_sem.at[tile, part], device_id={"cp": dev}, device_id_type=MESH)

    def h_copy(i):
        rows = pl.ds(i * half_tok, half_tok)
        return pltpu.make_async_remote_copy(
            src_ref=h2.at[0, rows, :], dst_ref=h2.at[1, rows, :], send_sem=hs_sem.at[i],
            recv_sem=hr_sem.at[i], device_id={"cp": partner}, device_id_type=MESH)

    def p_copy(n):
        return pltpu.make_async_remote_copy(
            src_ref=psend.at[n], dst_ref=precv.at[n], send_sem=ps_sem.at[n],
            recv_sem=pr_sem.at[n], device_id={"cp": partner}, device_id_type=MESH)

    for pos in range(NA):
        a_copy(0, pos).start()
    for q in range(ahead_b):
        for t in range(2):
            (up_copy(0, q, t) if q < n_up else dn_copy(0, q - n_up, t)).start()

    barrier = pltpu.get_barrier_semaphore()
    for dev in (up, dn, partner):
        pl.semaphore_signal(barrier, inc=1, device_id={"cp": dev}, device_id_type=MESH)

    xs[...] = x_in[...]
    qx[...] = jnp.zeros_like(qx)
    for i in range(n_layers):
        gains[0, i, 0:1, :] = g1_in[i:i + 1, :].astype(F32)
        gains[1, i, 0:1, :] = g2_in[i:i + 1, :].astype(F32)
    pl.semaphore_wait(barrier, 3)

    blk = 16

    def norm_rows(gain, first, count):
        def one(r, carry):
            rows = pl.ds(pl.multiple_of(first + r * blk, blk), blk)
            v = xs[rows, :].astype(F32)
            inv = lax.rsqrt(jnp.mean(v * v, axis=-1, keepdims=True) + NORM_EPS)
            h2[0, rows, :] = (v * inv * gain).astype(BF16)
            return carry

        lax.fori_loop(0, count // blk, one, 0, unroll=2)

    def rope_t(t):
        cos_b = cos_in[...]
        sin_b = sin_in[...]
        outs = []
        for n in range(t.shape[0] // head_dim):
            a = t[n * head_dim:n * head_dim + half]
            b = t[n * head_dim + half:(n + 1) * head_dim]
            outs.append(a * cos_b - b * sin_b)
            outs.append(b * cos_b + a * sin_b)
        return outs

    def fronts(parts):
        return jnp.concatenate([p[:, :half_tok] for p in parts], axis=1)

    def backs(parts):
        return jnp.concatenate([p[:, half_tok:] for p in parts], axis=1)

    n_unit = 2 * n_chip
    lane = lax.rem(lax.broadcasted_iota(jnp.int32, (1, n_tok), 1), half_tok)
    nat_qs = (me * half_tok + lane, (2 * n_cp - 1 - me) * half_tok + lane)

    def retile(chip):
        step_r = 256
        for r in range(0, 2 * kvw, step_r):
            t0 = kv[chip * 2, r:r + step_r, :]
            t1 = kv[chip * 2 + 1, r:r + step_r, :]
            kvt[r:r + step_r, :n_tok] = fronts([t0, t1])
            kvt[r:r + step_r, n_tok:] = backs([t1, t0])

    def cache_cols(chip):
        r0 = pl.multiple_of(me * n_col, n_col)
        for t in range(2):
            rows = kvt[pl.ds(t * kvw + r0, n_col), :]
            cbuf[t, :, pl.ds(pl.multiple_of(chip * n_tok, n_tok), n_tok)] = rows[:, :n_tok]
            cbuf[t, :, pl.ds(pl.multiple_of((n_unit - 1 - chip) * n_tok, n_tok), n_tok)] = rows[:, n_tok:]

    def attend(chip, blocks):
        retile(chip)
        cache_cols(chip)
        units = max(u for _, u in blocks)
        for p in range(n_kv // 2):
            rows = slice(p * 2 * head_dim, (p + 1) * 2 * head_dim)
            for u in range(units):
                knat[p, u * n_tok:(u + 1) * n_tok, :] = kvt[rows, u * n_tok:(u + 1) * n_tok].T
        key = lax.broadcasted_iota(jnp.int32, (n_tok, n_tok), 0)
        for qh, n_u in blocks:
            start_q = nat_qs[qh] - pos_in[qh:qh + 1, :]
            for u in range(n_u):
                nat_k = (chip if u == 0 else n_unit - 1 - chip) * n_tok + key
                ok = (nat_k >= start_q) & (nat_k <= nat_qs[qh])
                cap[qh, u * n_tok:(u + 1) * n_tok, :] = jnp.where(ok, BIG, MASK_FILL)

        jobs = [(g, qh, n_u * n_tok) for g in range(n_kv) for qh, n_u in blocks]

        def scores(g, qh, n_k):
            return jnp.dot(knat[g // 2, :n_k, :], qx[g, :, qh * lane_f:(qh + 1) * lane_f], preferred_element_type=F32)

        ahead = [scores(*job) for job in jobs[:AHEAD]]
        for n, (g, qh, n_k) in enumerate(jobs):
            ls = slice(qh * lane_f, (qh + 1) * lane_f)
            capv = cap[qh, :n_k, :]
            capv = jnp.concatenate([capv] * (lane_f // n_tok), axis=1)
            s_t = jnp.minimum(ahead.pop(0), capv) * LOG2E
            if n + AHEAD < len(jobs):
                ahead.append(scores(*jobs[n + AHEAD]))
            m_old = m_st[g, 0:1, ls]
            m_new = jnp.maximum(m_old, jnp.max(s_t, axis=0, keepdims=True))
            e = jnp.exp2(s_t - m_new)
            alpha = jnp.exp2(m_old - m_new)
            m_st[g, 0:1, ls] = m_new
            l_st[g, 0:1, ls] = l_st[g, 0:1, ls] * alpha + jnp.sum(e, axis=0, keepdims=True)
            rows = slice(kvw + g * head_dim, kvw + (g + 1) * head_dim)
            pv = jnp.dot(kvt[rows, :n_k], e.astype(BF16), preferred_element_type=F32)
            oacc[g, :, ls] = oacc[g, :, ls] * alpha + pv

    def tile_of(dist):
        return lax.rem(z + dist + n_chip, n_chip) * 2 + c

    far = n_chip // 2

    def serve(part, dist):
        lo, hi = tile_of(-dist), tile_of(dist)
        if dist < far or part == 0:
            ring_copy(UP, lo, part).wait_recv()
            if dist < far - 1 or (dist == far - 1 and part == 0):
                ring_copy(UP, lo, part).start()
            ring_copy(D2D, lo, part).start()
        if dist < far or part == 1:
            ring_copy(DN, hi, part).wait_recv()
            if dist < far - 1 or (dist == far - 1 and part == 1):
                ring_copy(DN, hi, part).start()
            ring_copy(D2D, hi, part).start()

    plan = {1: [(0, 1), (1, 1)]}
    for d in range(2, far):
        plan[2 * d - 2] = [(0, d)]
        plan[2 * d - 1] = [(1, d)]
    plan[2 * far - 2] = [(0, far), (1, far)]

    def layer(l, carry):
        has_next = l + 1 < n_layers

        norm_rows(gains[0, l, 0:1, :], 0, n_tok)

        @pl.when(l > 0)
        def _():
            for i in range(3):
                pl.semaphore_wait(cred.at[i], 1)

        for part in range(2):
            a_copy(l, part).wait()
            t = lax.dot_general(ring_a[a_slot(l, part)], h2[0], NT, preferred_element_type=F32)
            if part == 0:
                for n, b in enumerate(rope_t(t)):
                    kv[me, n * half:(n + 1) * half, :] = b.astype(BF16)
            else:
                kv[me, kvw:2 * kvw, :] = t.astype(BF16)
            for dirn in (UP, DN, D2D):
                ring_copy(dirn, me, part).start()
            a_refill(l, part)

        for i in range(n_q):
            pos = first_q + i
            a_copy(l, pos).wait()
            t = lax.dot_general(ring_a[a_slot(l, pos)], h2[0], NT, preferred_element_type=F32)
            outs = [(b.astype(BF16).astype(F32) * head_dim ** -0.5).astype(BF16) for b in rope_t(t)]
            n_g = rows_a // (q_group * head_dim)
            for gg in range(n_g):
                g = i * n_g + gg
                for hb in range(2):
                    parts = [outs[2 * (gg * q_group + hh) + hb] for hh in range(q_group)]
                    r0 = (g % 2) * head_dim + hb * half
                    qx[g, r0:r0 + half, :lane_f] = fronts(parts)
                    qx[g, r0:r0 + half, lane_f:] = backs(parts)
            a_refill(l, pos)

        m_st[...] = jnp.full_like(m_st, MASK_FILL * LOG2E)
        l_st[...] = jnp.zeros_like(l_st)
        oacc[...] = jnp.zeros_like(oacc)

        for part in range(2):
            ring_copy(D2D, partner, part).wait_recv()
        attend(z, [(0, 1), (1, 2)])

        def step(k, carry):
            dist = (k + 1) // 2
            for at, todo in plan.items():
                @pl.when(k == at)
                def _():
                    for part, d in todo:
                        serve(part, d)
            chip = jnp.where(k % 2 == 1, z - dist + n_chip, z + dist) % n_chip
            other = chip * 2 + 1 - c
            for part in range(2):
                ring_copy(D2D, other, part).wait_recv()

            @pl.when(chip < z)
            def _():
                attend(chip, [(0, 1), (1, 1)])

            @pl.when(chip > z)
            def _():
                attend(chip, [(1, 2)])

            return carry

        lax.fori_loop(1, n_chip, step, 0)

        ck = pltpu.make_async_copy(cbuf.at[0], kc.at[l], csem.at[0])
        cv = pltpu.make_async_copy(cbuf.at[1], vc.at[l], csem.at[1])
        ck.start()
        cv.start()

        for i in range(n_o):
            pos = first_o + i
            a_copy(l, pos).wait()
            n_g = rows_a // (q_group * head_dim)
            parts = []
            for gg in range(n_g):
                g = i * n_g + gg
                o = oacc[g] * (1.0 / l_st[g, 0:1, :])
                for hh in range(q_group):
                    f0 = hh * half_tok
                    parts.append(jnp.concatenate(
                        [o[:, f0:f0 + half_tok], o[:, lane_f + f0:lane_f + f0 + half_tok]], axis=1))
            o_n = jnp.concatenate(parts, axis=0).T.astype(BF16)
            y = jnp.dot(o_n, ring_a[a_slot(l, pos)], preferred_element_type=F32)
            if i == 0:
                acc[...] = y
            else:
                acc[...] += y
            a_refill(l, pos)

        gain = gains[1, l, 0:1, :]
        for i in range(2):
            def one(r, carry):
                rows = pl.ds(pl.multiple_of(i * half_tok + r * blk, blk), blk)
                xs[rows, :] = (xs[rows, :].astype(F32) + acc[rows, :]).astype(BF16)
                return carry

            lax.fori_loop(0, half_tok // blk, one, 0, unroll=2)
            norm_rows(gain, i * half_tok, half_tok)
            h_copy(i).start()

        ck.wait()
        cv.wait()
        for part in range(2):
            for dirn in (UP, DN, D2D):
                ring_copy(dirn, me, part).wait_send()
            for dist in range(1, far):
                lo, hi = tile_of(-dist), tile_of(dist)
                if dist < far - 1 or part == 0:
                    ring_copy(UP, lo, part).wait_send()
                if dist < far - 1 or part == 1:
                    ring_copy(DN, hi, part).wait_send()
                ring_copy(D2D, lo, part).wait_send()
                ring_copy(D2D, hi, part).wait_send()
            ring_copy(D2D, tile_of(far), part).wait_send()

        @pl.when(has_next)
        def _():
            pl.semaphore_signal(cred.at[DN], inc=1, device_id={"cp": up}, device_id_type=MESH)
            pl.semaphore_signal(cred.at[UP], inc=1, device_id={"cp": dn}, device_id_type=MESH)
            pl.semaphore_signal(cred.at[D2D], inc=1, device_id={"cp": partner}, device_id_type=MESH)

        for i in range(2):
            h_copy(i).wait_recv()

        def up_step(j, carry):
            for t in range(2):
                up_copy(l, j, t).wait()
            h_all = h2[...].reshape(2 * n_tok, d_model)
            a = jnp.dot(h_all, ring_b[b_slot(l, j, 0)], preferred_element_type=F32)
            b = jnp.dot(h_all, ring_b[b_slot(l, j, 1)], preferred_element_type=F32)
            ub[:, pl.ds(pl.multiple_of(j * cols_b, cols_b), cols_b)] = (jax.nn.silu(a) * b).astype(BF16)
            b_refill(l, j)
            return carry

        lax.fori_loop(0, n_up, up_step, 0)

        def dn_step(n, carry):
            for t in range(2):
                dn_copy(l, n, t).wait()
            y = jnp.dot(ub[:, :k_b], ring_b[b_slot(l, n_up + n, 0)], preferred_element_type=F32)
            y += jnp.dot(ub[:, k_b:], ring_b[b_slot(l, n_up + n, 1)], preferred_element_type=F32)
            psend[n] = y[n_tok:]
            p_copy(n).start()
            acc[:, pl.ds(pl.multiple_of(n * cols_b, cols_b), cols_b)] = y[:n_tok]
            b_refill(l, n_up + n)
            return carry

        lax.fori_loop(0, n_dn, dn_step, 0)
        for i in range(2):
            h_copy(i).wait_send()

        def merge(n, carry):
            p_copy(n).wait()
            cols = pl.ds(pl.multiple_of(n * cols_b, cols_b), cols_b)
            xs[:, cols] = (xs[:, cols].astype(F32) + (acc[:, cols] + precv[n])).astype(BF16)
            return carry

        lax.fori_loop(0, n_dn, merge, 0)
        return carry

    lax.fori_loop(0, n_layers, layer, 0)
    x_out[...] = xs[...]


def solution(mesh):
    n_cp = mesh.shape["cp"]
    row_spec = P(("req", "cp"), None)
    tok_spec = P(("req", "cp"))
    rep_spec = P()
    cache_spec = P(None, "req", "cp")

    def local_step(hidden, positions, segments, gain_1, gain_2, w_q, w_k, w_v, w_o, w_1, w_3, w_2):
        n_layers, d_model, n_heads, head_dim = w_q.shape
        n_kv = w_k.shape[2]
        n_tok = hidden.shape[0]
        kvw = n_kv * head_dim
        q_group = n_heads // n_kv
        d_ff = w_1.shape[2]
        rows_a, cols_b, k_b, nb = kvw, d_model // 4, d_ff // 4, NB
        inv_freq = ROPE_THETA ** (-2.0 * jnp.arange(head_dim // 2, dtype=F32) / head_dim)
        angle = inv_freq[:, None] * positions.astype(F32)[None, :]
        cos_t, sin_t = jnp.cos(angle), jnp.sin(angle)
        pos_2 = positions.reshape(2, n_tok // 2)
        pos_2 = jnp.concatenate([pos_2, pos_2], axis=1)

        def turned(w):
            return jnp.transpose(w, (0, 2, 3, 1)).reshape(n_layers, -1, d_model)

        cfg = dict(layers=n_layers, n_cp=n_cp, nb=nb)
        vmem = pl.BlockSpec(memory_space=pltpu.VMEM)
        hbm = pl.BlockSpec(memory_space=pl.ANY)
        n_all = n_cp * n_tok
        cache = jax.ShapeDtypeStruct((n_layers, kvw // n_cp, n_all), BF16)
        x, k_c, v_c = pl.pallas_call(
            functools.partial(kernel, cfg),
            out_shape=(jax.ShapeDtypeStruct(hidden.shape, BF16), cache, cache),
            in_specs=[vmem] * 6 + [hbm] * 7,
            out_specs=(vmem, hbm, hbm),
            scratch_shapes=[
                pltpu.VMEM((NA, rows_a, d_model), BF16),
                pltpu.VMEM((nb, k_b, cols_b), BF16),
                pltpu.VMEM((n_cp, 2 * kvw, n_tok), BF16),
                pltpu.VMEM((2 * kvw, 2 * n_tok), BF16),
                pltpu.VMEM((n_kv // 2, 2 * n_tok, 2 * head_dim), BF16),
                pltpu.VMEM((n_kv, 2 * head_dim, q_group * n_tok), BF16),
                pltpu.VMEM((n_kv, head_dim, q_group * n_tok), F32),
                pltpu.VMEM((n_kv, 8, q_group * n_tok), F32),
                pltpu.VMEM((n_kv, 8, q_group * n_tok), F32),
                pltpu.VMEM((2, 2 * n_tok, n_tok), F32),
                pltpu.VMEM((2, kvw // n_cp, n_all), BF16),
                pltpu.VMEM((n_tok, d_model), BF16),
                pltpu.VMEM((2, n_tok, d_model), BF16),
                pltpu.VMEM((2 * n_tok, d_ff // 2), BF16),
                pltpu.VMEM((n_tok, d_model), F32),
                pltpu.VMEM((d_model // cols_b, n_tok, cols_b), F32),
                pltpu.VMEM((d_model // cols_b, n_tok, cols_b), F32),
                pltpu.VMEM((2, n_layers, 8, d_model), F32),
                pltpu.SemaphoreType.DMA((NA,)),
                pltpu.SemaphoreType.DMA((nb,)),
                pltpu.SemaphoreType.DMA((3, n_cp, 2)),
                pltpu.SemaphoreType.DMA((n_cp, 2)),
                pltpu.SemaphoreType.DMA((2,)),
                pltpu.SemaphoreType.DMA((2,)),
                pltpu.SemaphoreType.DMA((d_model // cols_b,)),
                pltpu.SemaphoreType.DMA((d_model // cols_b,)),
                pltpu.SemaphoreType.REGULAR((3,)),
                pltpu.SemaphoreType.DMA((2,)),
            ],
            compiler_params=pltpu.CompilerParams(
                collective_id=0, has_side_effects=True, vmem_limit_bytes=67043328),
            name="prefill",
        )(
            hidden, pos_2, cos_t, sin_t, gain_1, gain_2,
            turned(w_q), turned(w_k), turned(w_v), w_o.reshape(n_layers, -1, d_model), w_1, w_3, w_2,
        )
        return x, jnp.transpose(k_c, (0, 2, 1)), jnp.transpose(v_c, (0, 2, 1))

    return jax.shard_map(
        local_step,
        mesh=mesh,
        in_specs=(row_spec, tok_spec, tok_spec) + (rep_spec,) * 9,
        out_specs=(row_spec, cache_spec, cache_spec),
        check_vma=False,
    )
```

time: 254 us -> 183 us (0.72)
  Pallas kernels: 235 us -> 174 us
  local copies, waits for them, and re-layouts: 16.3 us -> 6.15 us
    pallas_call x1, Pallas kernels: 235 us -> 174 us  [local_step(): pl.pallas_call(functools.partial(kernel, cfg), out_shape=(jax.ShapeDtypeS...]
    reshape x4 -> x1, local copies, waits for them, and re-layouts: 7.22 us -> 0.74 us  [local_step(): pos_2 = positions.reshape(2, n_tok // 2)]
    unnamed x1 -> x3, local copies, waits for them, and re-layouts: 1.88 us -> 5.41 us
    slice x2 -> x0, local copies, waits for them, and re-layouts: 3.49 us -> none  [to_natural(): front = blocks[:, :, :, 0]]
    broadcast_in_dim x2 -> x0, local copies, waits for them, and re-layouts: 2.68 us -> none  [the longest x1 1.34 us: local_step(): gain_1.astype(F32)[:, None, :]]
where the time goes in v2:
time: 183 us
  Pallas kernels  174 us (95%)
  local copies, waits for them, and re-layouts  6.15 us (3%)
  other arithmetic  2.06 us (1%)
    pallas_call x1, Pallas kernels, local_step(): pl.pallas_call(functools.partial(kernel, cfg), out_shape=(jax.ShapeDtypeS...  174 us
    unnamed x3, local copies, waits for them, and re-layouts  5.41 us

profile of v2, /device:TPU:21, one launch (start us, length us, event | category | flops | bytes accessed | tf_op | source)
XLA Modules:
  0.0 183.2 jit_solution(2802890443178250145)
XLA Ops:
  0.6 0.7 convert_element_type.3
  1.3 0.7 reshape.27
  2.0 0.6 pad_add_fusion.pos_in
  2.7 0.8 multiply_sine_fusion
  3.4 174.3 %prefill.1 = (bf16[128,2048]{1,0:T(8,128)(2,1)}, bf16[3,32,2048]{2,1,0:T(8,128)(2,1)}, bf16[3,32,2048]{2,1,0:T(8,128)(2,1)}) custom-call(bf16[128,2048]{1,0:T(8,128)(2,1)} %x_in.1, s32[2,128]{1,0:T(2,128)} %pad_add_fusion.pos_in, f32[32,128]{1,0:T(8,128)} %get-tuple-element.10.cos_in, f32[32,128]{1,0:T(8,128)} %get-tuple-element.9.sin_in, ...), custom_call_target="tpu_custom_call" | custom-call | tf_op jit(solution)/shard_map/prefill/pallas_call | solution.py:457
  177.8 1.9 %copy.17 = bf16[128,2048]{1,0:T(8,128)(2,1)} copy(bf16[128,2048]{1,0:T(8,128)(2,1)} %get-tuple-element.14) | data formatting | bytes 1048576
  179.6 1.8 copy.18
  181.4 1.8 copy.19
  (1 shorter events, 0.0 us)

commit v3 on v2

--- a/solution.py
+++ b/solution.py
@@ -25,8 +25,8 @@
 
 def kernel(cfg, x_in, pos_in, cos_in, sin_in, g1_in, g2_in, wq, wk, wv, wo, w1, w3, w2,
            x_out, kc, vc,
-           ring_a, ring_b, kv, kvt, knat, qx, oacc, m_st, l_st, cap, cbuf, xs, h2, ub, acc, psend, precv, gains,
-           sem_a, sem_b, send_sem, recv_sem, hs_sem, hr_sem, ps_sem, pr_sem, cred, csem):
+           ring_a, ring_b, kv, kvt, knat, qx, oacc, m_st, l_st, cap, cbuf, o_n, xs, h2, ub, acc, psend, precv, gains,
+           sem_a, sem_b, send_sem, recv_sem, fs_sem, fr_sem, hs_sem, hr_sem, ps_sem, pr_sem, cred, csem):
     n_layers, n_cp, nb = cfg["layers"], cfg["n_cp"], cfg["nb"]
     n_tok, d_model = xs.shape
     half_tok = n_tok // 2
@@ -117,6 +117,12 @@
             src_ref=ref, dst_ref=ref, send_sem=send_sem.at[dirn, tile, part],
             recv_sem=recv_sem.at[tile, part], device_id={"cp": dev}, device_id_type=MESH)
 
+    def far_copy(dirn, tile, part):
+        ref = kv.at[tile, pl.ds(part * kvw + dirn * (kvw // 2), kvw // 2), :]
+        return pltpu.make_async_remote_copy(
+            src_ref=ref, dst_ref=ref, send_sem=fs_sem.at[dirn, part],
+            recv_sem=fr_sem.at[dirn, part], device_id={"cp": (up, dn)[dirn]}, device_id_type=MESH)
+
     def h_copy(i):
         rows = pl.ds(i * half_tok, half_tok)
         return pltpu.make_async_remote_copy(
@@ -130,10 +136,6 @@
 
     for pos in range(NA):
         a_copy(0, pos).start()
-    for q in range(ahead_b):
-        for t in range(2):
-            (up_copy(0, q, t) if q < n_up else dn_copy(0, q - n_up, t)).start()
-
     barrier = pltpu.get_barrier_semaphore()
     for dev in (up, dn, partner):
         pl.semaphore_signal(barrier, inc=1, device_id={"cp": dev}, device_id_type=MESH)
@@ -167,6 +169,10 @@
             outs.append(a * cos_b - b * sin_b)
             outs.append(b * cos_b + a * sin_b)
         return outs
+
+    def project(ref):
+        mid = rows_a // 2
+        return [lax.dot_general(ref[i * mid:(i + 1) * mid, :], h2[0], NT, preferred_element_type=F32) for i in range(2)]
 
     def fronts(parts):
         return jnp.concatenate([p[:, :half_tok] for p in parts], axis=1)
@@ -239,16 +245,18 @@
 
     def serve(part, dist):
         lo, hi = tile_of(-dist), tile_of(dist)
-        if dist < far or part == 0:
-            ring_copy(UP, lo, part).wait_recv()
-            if dist < far - 1 or (dist == far - 1 and part == 0):
-                ring_copy(UP, lo, part).start()
-            ring_copy(D2D, lo, part).start()
-        if dist < far or part == 1:
-            ring_copy(DN, hi, part).wait_recv()
-            if dist < far - 1 or (dist == far - 1 and part == 1):
-                ring_copy(DN, hi, part).start()
+        if dist == far:
+            for dirn in (UP, DN):
+                far_copy(dirn, hi, part).wait_recv()
             ring_copy(D2D, hi, part).start()
+            return
+        for dirn, tile in ((UP, lo), (DN, hi)):
+            ring_copy(dirn, tile, part).wait_recv()
+            if dist < far - 1:
+                ring_copy(dirn, tile, part).start()
+            else:
+                far_copy(dirn, tile, part).start()
+            ring_copy(D2D, tile, part).start()
 
     plan = {1: [(0, 1), (1, 1)]}
     for d in range(2, far):
@@ -268,30 +276,39 @@
 
         for part in range(2):
             a_copy(l, part).wait()
-            t = lax.dot_general(ring_a[a_slot(l, part)], h2[0], NT, preferred_element_type=F32)
+            ts = project(ring_a.at[a_slot(l, part)])
             if part == 0:
-                for n, b in enumerate(rope_t(t)):
+                for n, b in enumerate(rope_t(ts[0]) + rope_t(ts[1])):
                     kv[me, n * half:(n + 1) * half, :] = b.astype(BF16)
             else:
-                kv[me, kvw:2 * kvw, :] = t.astype(BF16)
+                kv[me, kvw:kvw + kvw // 2, :] = ts[0].astype(BF16)
+                kv[me, kvw + kvw // 2:2 * kvw, :] = ts[1].astype(BF16)
             for dirn in (UP, DN, D2D):
                 ring_copy(dirn, me, part).start()
             a_refill(l, part)
 
-        for i in range(n_q):
-            pos = first_q + i
-            a_copy(l, pos).wait()
-            t = lax.dot_general(ring_a[a_slot(l, pos)], h2[0], NT, preferred_element_type=F32)
-            outs = [(b.astype(BF16).astype(F32) * head_dim ** -0.5).astype(BF16) for b in rope_t(t)]
-            n_g = rows_a // (q_group * head_dim)
-            for gg in range(n_g):
-                g = i * n_g + gg
-                for hb in range(2):
-                    parts = [outs[2 * (gg * q_group + hh) + hb] for hh in range(q_group)]
-                    r0 = (g % 2) * head_dim + hb * half
-                    qx[g, r0:r0 + half, :lane_f] = fronts(parts)
-                    qx[g, r0:r0 + half, lane_f:] = backs(parts)
-            a_refill(l, pos)
+        @pl.when(l == 0)
+        def _():
+            for q in range(ahead_b):
+                for t in range(2):
+                    (up_copy(0, q, t) if q < n_up else dn_copy(0, q - n_up, t)).start()
+
+        for i0 in range(0, n_q, 2):
+            for i in (i0, i0 + 1):
+                a_copy(l, first_q + i).wait()
+            for i in (i0, i0 + 1):
+                ts = project(ring_a.at[a_slot(l, first_q + i)])
+                outs = [(b.astype(BF16).astype(F32) * head_dim ** -0.5).astype(BF16) for b in rope_t(ts[0]) + rope_t(ts[1])]
+                n_g = rows_a // (q_group * head_dim)
+                for gg in range(n_g):
+                    g = i * n_g + gg
+                    for hb in range(2):
+                        parts = [outs[2 * (gg * q_group + hh) + hb] for hh in range(q_group)]
+                        r0 = (g % 2) * head_dim + hb * half
+                        qx[g, r0:r0 + half, :lane_f] = fronts(parts)
+                        qx[g, r0:r0 + half, lane_f:] = backs(parts)
+            for i in (i0, i0 + 1):
+                a_refill(l, first_q + i)
 
         m_st[...] = jnp.full_like(m_st, MASK_FILL * LOG2E)
         l_st[...] = jnp.zeros_like(l_st)
@@ -331,8 +348,9 @@
         cv.start()
 
         for i in range(n_o):
-            pos = first_o + i
-            a_copy(l, pos).wait()
+            a_copy(l, first_o + i).wait()
+        y = None
+        for i in range(n_o):
             n_g = rows_a // (q_group * head_dim)
             parts = []
             for gg in range(n_g):
@@ -342,13 +360,16 @@
                     f0 = hh * half_tok
                     parts.append(jnp.concatenate(
                         [o[:, f0:f0 + half_tok], o[:, lane_f + f0:lane_f + f0 + half_tok]], axis=1))
-            o_n = jnp.concatenate(parts, axis=0).T.astype(BF16)
-            y = jnp.dot(o_n, ring_a[a_slot(l, pos)], preferred_element_type=F32)
-            if i == 0:
-                acc[...] = y
-            else:
-                acc[...] += y
-            a_refill(l, pos)
+            o_n[:, i * rows_a:(i + 1) * rows_a] = jnp.concatenate(parts, axis=0).T.astype(BF16)
+        for j in range(n_dn):
+            cols = slice(j * cols_b, (j + 1) * cols_b)
+            y = None
+            for i in range(n_o):
+                t = jnp.dot(o_n[:, i * rows_a:(i + 1) * rows_a], ring_a[a_slot(l, first_o + i), :, cols], preferred_element_type=F32)
+                y = t if y is None else y + t
+            acc[:, cols] = y
+        for i in range(n_o):
+            a_refill(l, first_o + i)
 
         gain = gains[1, l, 0:1, :]
         for i in range(2):
@@ -367,13 +388,12 @@
             for dirn in (UP, DN, D2D):
                 ring_copy(dirn, me, part).wait_send()
             for dist in range(1, far):
-                lo, hi = tile_of(-dist), tile_of(dist)
-                if dist < far - 1 or part == 0:
-                    ring_copy(UP, lo, part).wait_send()
-                if dist < far - 1 or part == 1:
-                    ring_copy(DN, hi, part).wait_send()
-                ring_copy(D2D, lo, part).wait_send()
-                ring_copy(D2D, hi, part).wait_send()
+                for dirn, tile in ((UP, tile_of(-dist)), (DN, tile_of(dist))):
+                    if dist < far - 1:
+                        ring_copy(dirn, tile, part).wait_send()
+                    else:
+                        far_copy(dirn, tile, part).wait_send()
+                    ring_copy(D2D, tile, part).wait_send()
             ring_copy(D2D, tile_of(far), part).wait_send()
 
         @pl.when(has_next)
@@ -385,17 +405,21 @@
         for i in range(2):
             h_copy(i).wait_recv()
 
-        def up_step(j, carry):
-            for t in range(2):
-                up_copy(l, j, t).wait()
+        def up_step(j0, carry):
+            js = (2 * j0, 2 * j0 + 1)
+            for j in js:
+                for t in range(2):
+                    up_copy(l, j, t).wait()
             h_all = h2[...].reshape(2 * n_tok, d_model)
-            a = jnp.dot(h_all, ring_b[b_slot(l, j, 0)], preferred_element_type=F32)
-            b = jnp.dot(h_all, ring_b[b_slot(l, j, 1)], preferred_element_type=F32)
-            ub[:, pl.ds(pl.multiple_of(j * cols_b, cols_b), cols_b)] = (jax.nn.silu(a) * b).astype(BF16)
-            b_refill(l, j)
+            for j in js:
+                a = jnp.dot(h_all, ring_b[b_slot(l, j, 0)], preferred_element_type=F32)
+                b = jnp.dot(h_all, ring_b[b_slot(l, j, 1)], preferred_element_type=F32)
+                ub[:, pl.ds(pl.multiple_of(j * cols_b, cols_b), cols_b)] = (jax.nn.silu(a) * b).astype(BF16)
+            for j in js:
+                b_refill(l, j)
             return carry
 
-        lax.fori_loop(0, n_up, up_step, 0)
+        lax.fori_loop(0, n_up // 2, up_step, 0)
 
         def dn_step(n, carry):
             for t in range(2):
@@ -471,6 +495,7 @@
                 pltpu.VMEM((n_kv, 8, q_group * n_tok), F32),
                 pltpu.VMEM((2, 2 * n_tok, n_tok), F32),
                 pltpu.VMEM((2, kvw // n_cp, n_all), BF16),
+                pltpu.VMEM((n_tok, n_heads * head_dim), BF16),
                 pltpu.VMEM((n_tok, d_model), BF16),
                 pltpu.VMEM((2, n_tok, d_model), BF16),
                 pltpu.VMEM((2 * n_tok, d_ff // 2), BF16),
@@ -482,6 +507,8 @@
                 pltpu.SemaphoreType.DMA((nb,)),
                 pltpu.SemaphoreType.DMA((3, n_cp, 2)),
                 pltpu.SemaphoreType.DMA((n_cp, 2)),
+                pltpu.SemaphoreType.DMA((2, 2)),
+                pltpu.SemaphoreType.DMA((2, 2)),
                 pltpu.SemaphoreType.DMA((2,)),
                 pltpu.SemaphoreType.DMA((2,)),
                 pltpu.SemaphoreType.DMA((d_model // cols_b,)),

time: 183 us -> 171 us (0.934)
  Pallas kernels: 174 us -> 162 us
    pallas_call x1, Pallas kernels: 174 us -> 162 us  [local_step(): pl.pallas_call(functools.partial(kernel, cfg), out_shape=(jax.ShapeDtypeS...]
where the time goes in v3:
time: 171 us
  Pallas kernels  162 us (95%)
  local copies, waits for them, and re-layouts  6.15 us (4%)
  other arithmetic  2.06 us (1%)
    pallas_call x1, Pallas kernels, local_step(): pl.pallas_call(functools.partial(kernel, cfg), out_shape=(jax.ShapeDtypeS...  162 us
    unnamed x3, local copies, waits for them, and re-layouts  5.41 us

profile of v3, /device:TPU:21, one launch (start us, length us, event | category | flops | bytes accessed | tf_op | source)
XLA Modules:
  0.0 171.1 jit_solution(5778876098734585744)
XLA Ops:
  0.6 0.7 convert_element_type.3
  1.3 0.7 reshape.27
  2.0 0.6 pad_add_fusion.pos_in
  2.7 0.8 multiply_sine_fusion
  3.4 162.2 %prefill.1 = (bf16[128,2048]{1,0:T(8,128)(2,1)}, bf16[3,32,2048]{2,1,0:T(8,128)(2,1)}, bf16[3,32,2048]{2,1,0:T(8,128)(2,1)}) custom-call(bf16[128,2048]{1,0:T(8,128)(2,1)} %x_in.1, s32[2,128]{1,0:T(2,128)} %pad_add_fusion.pos_in, f32[32,128]{1,0:T(8,128)} %get-tuple-element.10.cos_in, f32[32,128]{1,0:T(8,128)} %get-tuple-element.9.sin_in, ...), custom_call_target="tpu_custom_call" | custom-call | tf_op jit(solution)/shard_map/prefill/pallas_call | solution.py:481
  165.6 1.9 %copy.17 = bf16[128,2048]{1,0:T(8,128)(2,1)} copy(bf16[128,2048]{1,0:T(8,128)(2,1)} %get-tuple-element.14) | data formatting | bytes 1048576
  167.5 1.8 %copy.18 = bf16[3,2048,32]{1,2,0:T(8,128)(2,1)} copy(bf16[3,2048,32]{1,2,0:T(8,128)(2,1)} %bitcast.17) | data formatting | bytes 786432
  169.3 1.8 %copy.19 = bf16[3,2048,32]{1,2,0:T(8,128)(2,1)} copy(bf16[3,2048,32]{1,2,0:T(8,128)(2,1)} %bitcast.16) | data formatting | bytes 786432
  (1 shorter events, 0.0 us)

commit v4 on v3

--- a/solution.py
+++ b/solution.py
@@ -134,18 +134,19 @@
             src_ref=psend.at[n], dst_ref=precv.at[n], send_sem=ps_sem.at[n],
             recv_sem=pr_sem.at[n], device_id={"cp": partner}, device_id_type=MESH)
 
+    pltpu.make_async_copy(x_in, xs, csem.at[0]).start()
     for pos in range(NA):
         a_copy(0, pos).start()
     barrier = pltpu.get_barrier_semaphore()
     for dev in (up, dn, partner):
         pl.semaphore_signal(barrier, inc=1, device_id={"cp": dev}, device_id_type=MESH)
 
-    xs[...] = x_in[...]
     qx[...] = jnp.zeros_like(qx)
     for i in range(n_layers):
         gains[0, i, 0:1, :] = g1_in[i:i + 1, :].astype(F32)
         gains[1, i, 0:1, :] = g2_in[i:i + 1, :].astype(F32)
     pl.semaphore_wait(barrier, 3)
+    pltpu.make_async_copy(x_in, xs, csem.at[0]).wait()
 
     blk = 16
 
@@ -209,7 +210,8 @@
                 knat[p, u * n_tok:(u + 1) * n_tok, :] = kvt[rows, u * n_tok:(u + 1) * n_tok].T
         key = lax.broadcasted_iota(jnp.int32, (n_tok, n_tok), 0)
         for qh, n_u in blocks:
-            start_q = nat_qs[qh] - pos_in[qh:qh + 1, :]
+            pos_q = pos_in[:, qh * half_tok:(qh + 1) * half_tok]
+            start_q = nat_qs[qh] - jnp.concatenate([pos_q, pos_q], axis=1)
             for u in range(n_u):
                 nat_k = (chip if u == 0 else n_unit - 1 - chip) * n_tok + key
                 ok = (nat_k >= start_q) & (nat_k <= nat_qs[qh])
@@ -402,51 +404,89 @@
             pl.semaphore_signal(cred.at[UP], inc=1, device_id={"cp": dn}, device_id_type=MESH)
             pl.semaphore_signal(cred.at[D2D], inc=1, device_id={"cp": partner}, device_id_type=MESH)
 
-        for i in range(2):
-            h_copy(i).wait_recv()
+        def up_dots(h_rows, rows, js):
+            for j in js:
+                a = jnp.dot(h_rows, ring_b[b_slot(l, j, 0)], preferred_element_type=F32)
+                b = jnp.dot(h_rows, ring_b[b_slot(l, j, 1)], preferred_element_type=F32)
+                ub[rows, pl.ds(pl.multiple_of(j * cols_b, cols_b), cols_b)] = (jax.nn.silu(a) * b).astype(BF16)
 
         def up_step(j0, carry):
             js = (2 * j0, 2 * j0 + 1)
             for j in js:
                 for t in range(2):
                     up_copy(l, j, t).wait()
-            h_all = h2[...].reshape(2 * n_tok, d_model)
-            for j in js:
-                a = jnp.dot(h_all, ring_b[b_slot(l, j, 0)], preferred_element_type=F32)
-                b = jnp.dot(h_all, ring_b[b_slot(l, j, 1)], preferred_element_type=F32)
-                ub[:, pl.ds(pl.multiple_of(j * cols_b, cols_b), cols_b)] = (jax.nn.silu(a) * b).astype(BF16)
+            up_dots(h2[...].reshape(2 * n_tok, d_model), slice(None), js)
             for j in js:
                 b_refill(l, j)
             return carry
 
-        lax.fori_loop(0, n_up // 2, up_step, 0)
+        for t in range(2):
+            up_copy(l, 0, t).wait()
+            up_copy(l, 1, t).wait()
+        up_dots(h2[0], slice(0, n_tok), (0, 1))
+        for i in range(2):
+            h_copy(i).wait_recv()
+        up_dots(h2[1], slice(n_tok, None), (0, 1))
+        for j in range(2):
+            b_refill(l, j)
+        lax.fori_loop(1, n_up // 2, up_step, 0)
+
+        def dn_dots(rows, n):
+            y = jnp.dot(ub[rows, :k_b], ring_b[b_slot(l, n_up + n, 0)], preferred_element_type=F32)
+            return y + jnp.dot(ub[rows, k_b:], ring_b[b_slot(l, n_up + n, 1)], preferred_element_type=F32)
+
+        def merge(n):
+            p_copy(n).wait()
+            cols = pl.ds(pl.multiple_of(n * cols_b, cols_b), cols_b)
+            xs[:, cols] = (xs[:, cols].astype(F32) + (acc[:, cols] + precv[n])).astype(BF16)
 
         def dn_step(n, carry):
             for t in range(2):
                 dn_copy(l, n, t).wait()
-            y = jnp.dot(ub[:, :k_b], ring_b[b_slot(l, n_up + n, 0)], preferred_element_type=F32)
-            y += jnp.dot(ub[:, k_b:], ring_b[b_slot(l, n_up + n, 1)], preferred_element_type=F32)
+            y = dn_dots(slice(None), n)
             psend[n] = y[n_tok:]
             p_copy(n).start()
             acc[:, pl.ds(pl.multiple_of(n * cols_b, cols_b), cols_b)] = y[:n_tok]
             b_refill(l, n_up + n)
+
+            @pl.when(n > 0)
+            def _():
+                merge(n - 1)
+
             return carry
 
-        lax.fori_loop(0, n_dn, dn_step, 0)
+        lax.fori_loop(0, n_dn - 1, dn_step, 0)
+
+        n = n_dn - 1
+        for t in range(2):
+            dn_copy(l, n, t).wait()
+        psend[n] = dn_dots(slice(n_tok, None), n)
+        p_copy(n).start()
+        acc[:, n * cols_b:] = dn_dots(slice(0, n_tok), n)
+        b_refill(l, n_up + n)
+        merge(n - 1)
         for i in range(2):
             h_copy(i).wait_send()
-
-        def merge(n, carry):
-            p_copy(n).wait()
-            cols = pl.ds(pl.multiple_of(n * cols_b, cols_b), cols_b)
-            xs[:, cols] = (xs[:, cols].astype(F32) + (acc[:, cols] + precv[n])).astype(BF16)
-            return carry
-
-        lax.fori_loop(0, n_dn, merge, 0)
+        merge(n)
         return carry
 
     lax.fori_loop(0, n_layers, layer, 0)
-    x_out[...] = xs[...]
+    out_copy = pltpu.make_async_copy(xs, x_out, csem.at[0])
+    out_copy.start()
+    out_copy.wait()
+
+
+def hand_over(*refs):
+    ins, outs, bufs, sem = refs[:3], refs[3:6], refs[6:9], refs[9]
+    first = [pltpu.make_async_copy(ins[i], bufs[i], sem.at[i]) for i in range(3)]
+    second = [pltpu.make_async_copy(bufs[i], outs[i], sem.at[i]) for i in range(3)]
+    for copy in first:
+        copy.start()
+    for i in range(3):
+        first[i].wait()
+        second[i].start()
+    for copy in second:
+        copy.wait()
 
 
 def solution(mesh):
@@ -467,8 +507,6 @@
         inv_freq = ROPE_THETA ** (-2.0 * jnp.arange(head_dim // 2, dtype=F32) / head_dim)
         angle = inv_freq[:, None] * positions.astype(F32)[None, :]
         cos_t, sin_t = jnp.cos(angle), jnp.sin(angle)
-        pos_2 = positions.reshape(2, n_tok // 2)
-        pos_2 = jnp.concatenate([pos_2, pos_2], axis=1)
 
         def turned(w):
             return jnp.transpose(w, (0, 2, 3, 1)).reshape(n_layers, -1, d_model)
@@ -481,8 +519,8 @@
         x, k_c, v_c = pl.pallas_call(
             functools.partial(kernel, cfg),
             out_shape=(jax.ShapeDtypeStruct(hidden.shape, BF16), cache, cache),
-            in_specs=[vmem] * 6 + [hbm] * 7,
-            out_specs=(vmem, hbm, hbm),
+            in_specs=[hbm] + [vmem] * 5 + [hbm] * 7,
+            out_specs=(hbm, hbm, hbm),
             scratch_shapes=[
                 pltpu.VMEM((NA, rows_a, d_model), BF16),
                 pltpu.VMEM((nb, k_b, cols_b), BF16),
@@ -520,9 +558,18 @@
                 collective_id=0, has_side_effects=True, vmem_limit_bytes=67043328),
             name="prefill",
         )(
-            hidden, pos_2, cos_t, sin_t, gain_1, gain_2,
+            hidden, positions[None, :], cos_t, sin_t, gain_1, gain_2,
             turned(w_q), turned(w_k), turned(w_v), w_o.reshape(n_layers, -1, d_model), w_1, w_3, w_2,
         )
+        results = (x, k_c, v_c)
+        x, k_c, v_c = pl.pallas_call(
+            hand_over,
+            out_shape=tuple(jax.ShapeDtypeStruct(r.shape, r.dtype) for r in results),
+            in_specs=[hbm] * 3,
+            out_specs=(hbm,) * 3,
+            scratch_shapes=[pltpu.VMEM(r.shape, r.dtype) for r in results] + [pltpu.SemaphoreType.DMA((3,))],
+            name="hand_over",
+        )(*results)
         return x, jnp.transpose(k_c, (0, 2, 1)), jnp.transpose(v_c, (0, 2, 1))
 
     return jax.shard_map(

time: 171 us -> 164 us (0.959)
  local copies, waits for them, and re-layouts: 6.15 us -> 0 us
    unnamed x3 -> x0, local copies, waits for them, and re-layouts: 5.41 us -> none
    pallas_call x1, Pallas kernels: 162 us -> 160 us  [local_step(): pl.pallas_call(functools.partial(kernel, cfg), out_shape=(jax.ShapeDtypeS...]
    pallas_call x0 -> x1, Pallas kernels: none -> 2.11 us  [local_step(): pl.pallas_call(hand_over, out_shape=tuple((jax.ShapeDtypeStruct(r.shape,...]
where the time goes in v4:
time: 164 us
  Pallas kernels  162 us (99%)
    pallas_call x1, Pallas kernels, local_step(): pl.pallas_call(functools.partial(kernel, cfg), out_shape=(jax.ShapeDtypeS...  160 us

profile of v4, /device:TPU:21, one launch (start us, length us, event | category | flops | bytes accessed | tf_op | source)
XLA Modules:
  0.0 164.0 jit_solution(16021018146977147862)
XLA Ops:
  0.6 0.7 convert_element_type.3
  1.3 0.8 multiply_sine_fusion
  2.1 159.8 %prefill.1 = (bf16[128,2048]{1,0:T(8,128)(2,1)}, bf16[3,32,2048]{2,1,0:T(8,128)(2,1)}, bf16[3,32,2048]{2,1,0:T(8,128)(2,1)}) custom-call(bf16[128,2048]{1,0:T(8,128)(2,1)} %x_in.1, s32[1,128]{1,0:T(1,128)} %bitcast.17, f32[32,128]{1,0:T(8,128)} %get-tuple-element.16.cos_in, f32[32,128]{1,0:T(8,128)} %get-tuple-element.15.sin_in, bf16[3,2048]{1,0:T(4,128)(2,1)} %g1_in.1, ...), custom_call_target="tpu_custom_call" | custom-call | tf_op jit(solution)/shard_map/prefill/pallas_call | solution.py:519
  161.9 2.1 %hand_over.1 = (bf16[128,2048]{1,0:T(8,128)(2,1)}, bf16[3,32,2048]{2,1,0:T(8,128)(2,1)}, bf16[3,32,2048]{2,1,0:T(8,128)(2,1)}) custom-call(bf16[128,2048]{1,0:T(8,128)(2,1)} %get-tuple-element.9.refs_0_, bf16[3,32,2048]{2,1,0:T(8,128)(2,1)} %get-tuple-element.10.refs_1_, bf16[3,32,2048]{2,1,0:T(8,128)(2,1)} %get-tuple-element.11.refs_2_), custom_call_target="tpu_custom_call" | custom-call | tf_op jit(solution)/shard_map/hand_over/pallas_call | solution.py:565
  (1 shorter events, 0.0 us)

commit v5 on v4

--- a/solution.py
+++ b/solution.py
@@ -185,25 +185,27 @@
     lane = lax.rem(lax.broadcasted_iota(jnp.int32, (1, n_tok), 1), half_tok)
     nat_qs = (me * half_tok + lane, (2 * n_cp - 1 - me) * half_tok + lane)
 
-    def retile(chip):
+    def retile(chip, units):
         step_r = 256
         for r in range(0, 2 * kvw, step_r):
             t0 = kv[chip * 2, r:r + step_r, :]
             t1 = kv[chip * 2 + 1, r:r + step_r, :]
             kvt[r:r + step_r, :n_tok] = fronts([t0, t1])
-            kvt[r:r + step_r, n_tok:] = backs([t1, t0])
+            if units == 2:
+                kvt[r:r + step_r, n_tok:] = backs([t1, t0])
 
     def cache_cols(chip):
         r0 = pl.multiple_of(me * n_col, n_col)
         for t in range(2):
-            rows = kvt[pl.ds(t * kvw + r0, n_col), :]
-            cbuf[t, :, pl.ds(pl.multiple_of(chip * n_tok, n_tok), n_tok)] = rows[:, :n_tok]
-            cbuf[t, :, pl.ds(pl.multiple_of((n_unit - 1 - chip) * n_tok, n_tok), n_tok)] = rows[:, n_tok:]
+            rows = pl.ds(t * kvw + r0, n_col)
+            t0, t1 = kv[chip * 2, rows, :], kv[chip * 2 + 1, rows, :]
+            cbuf[t, :, pl.ds(pl.multiple_of(chip * n_tok, n_tok), n_tok)] = fronts([t0, t1])
+            cbuf[t, :, pl.ds(pl.multiple_of((n_unit - 1 - chip) * n_tok, n_tok), n_tok)] = backs([t1, t0])
 
     def attend(chip, blocks):
-        retile(chip)
+        units = max(u for _, u in blocks)
+        retile(chip, units)
         cache_cols(chip)
-        units = max(u for _, u in blocks)
         for p in range(n_kv // 2):
             rows = slice(p * 2 * head_dim, (p + 1) * 2 * head_dim)
             for u in range(units):
@@ -222,14 +224,15 @@
         def scores(g, qh, n_k):
             return jnp.dot(knat[g // 2, :n_k, :], qx[g, :, qh * lane_f:(qh + 1) * lane_f], preferred_element_type=F32)
 
-        ahead = [scores(*job) for job in jobs[:AHEAD]]
+        lead = AHEAD * (2 if units == 1 else 1)
+        ahead = [scores(*job) for job in jobs[:lead]]
         for n, (g, qh, n_k) in enumerate(jobs):
             ls = slice(qh * lane_f, (qh + 1) * lane_f)
             capv = cap[qh, :n_k, :]
             capv = jnp.concatenate([capv] * (lane_f // n_tok), axis=1)
             s_t = jnp.minimum(ahead.pop(0), capv) * LOG2E
-            if n + AHEAD < len(jobs):
-                ahead.append(scores(*jobs[n + AHEAD]))
+            if n + lead < len(jobs):
+                ahead.append(scores(*jobs[n + lead]))
             m_old = m_st[g, 0:1, ls]
             m_new = jnp.maximum(m_old, jnp.max(s_t, axis=0, keepdims=True))
             e = jnp.exp2(s_t - m_new)
@@ -377,11 +380,14 @@
         for i in range(2):
             def one(r, carry):
                 rows = pl.ds(pl.multiple_of(i * half_tok + r * blk, blk), blk)
-                xs[rows, :] = (xs[rows, :].astype(F32) + acc[rows, :]).astype(BF16)
+                x_new = (xs[rows, :].astype(F32) + acc[rows, :]).astype(BF16)
+                xs[rows, :] = x_new
+                v = x_new.astype(F32)
+                inv = lax.rsqrt(jnp.mean(v * v, axis=-1, keepdims=True) + NORM_EPS)
+                h2[0, rows, :] = (v * inv * gain).astype(BF16)
                 return carry
 
             lax.fori_loop(0, half_tok // blk, one, 0, unroll=2)
-            norm_rows(gain, i * half_tok, half_tok)
             h_copy(i).start()
 
         ck.wait()

time: 164 us -> 163 us (level)
  no operation moved by 1% of the time
where the time goes in v5:
time: 163 us
  Pallas kernels  161 us (99%)
    pallas_call x1, Pallas kernels, local_step(): pl.pallas_call(functools.partial(kernel, cfg), out_shape=(jax.ShapeDtypeS...  159 us

profile of v5, /device:TPU:21, one launch (start us, length us, event | category | flops | bytes accessed | tf_op | source)
XLA Modules:
  0.0 162.9 jit_solution(4532890957530402364)
XLA Ops:
  0.6 0.7 convert_element_type.3
  1.3 0.8 multiply_sine_fusion
  2.1 158.7 %prefill.1 = (bf16[128,2048]{1,0:T(8,128)(2,1)}, bf16[3,32,2048]{2,1,0:T(8,128)(2,1)}, bf16[3,32,2048]{2,1,0:T(8,128)(2,1)}) custom-call(bf16[128,2048]{1,0:T(8,128)(2,1)} %x_in.1, s32[1,128]{1,0:T(1,128)} %bitcast.17, f32[32,128]{1,0:T(8,128)} %get-tuple-element.16.cos_in, f32[32,128]{1,0:T(8,128)} %get-tuple-element.15.sin_in, bf16[3,2048]{1,0:T(4,128)(2,1)} %g1_in.1, ...), custom_call_target="tpu_custom_call" | custom-call | tf_op jit(solution)/shard_map/prefill/pallas_call | solution.py:525
  160.8 2.1 %hand_over.1 = (bf16[128,2048]{1,0:T(8,128)(2,1)}, bf16[3,32,2048]{2,1,0:T(8,128)(2,1)}, bf16[3,32,2048]{2,1,0:T(8,128)(2,1)}) custom-call(bf16[128,2048]{1,0:T(8,128)(2,1)} %get-tuple-element.9.refs_0_, bf16[3,32,2048]{2,1,0:T(8,128)(2,1)} %get-tuple-element.10.refs_1_, bf16[3,32,2048]{2,1,0:T(8,128)(2,1)} %get-tuple-element.11.refs_2_), custom_call_target="tpu_custom_call" | custom-call | tf_op jit(solution)/shard_map/hand_over/pallas_call | solution.py:571
  (1 shorter events, 0.0 us)
